TPU v7x, 128 devices: a whole 4x4x4 slice. The times are simulated.
128 devices in a mesh: dp: 4 (over x_lo, core), ctx: 32 (over x_hi, y, z).
Axes of the slice: x: 4 (x_hi: 2, x_lo: 2; x = x_hi * 2 + x_lo), y: 4, z: 4, core: 2. Of those that a mesh axis runs over, the one named last changes fastest.
Arguments:
- tokens: bfloat16 [4, 16384, 2048], P('dp', 'ctx'), may hold values from -6 to 6
- in_weight: bfloat16 [2048, 5120], P(None, 'dp'), may hold values from -0.125 to 0.125
- step_weight: bfloat16 [2048, 64], replicated, may hold values from -0.125 to 0.125
- step_bias: float32 [64], replicated, may hold values from -3 to 0
- decay_rate: float32 [64], replicated, may hold values from 0.0001 to 0.5
- skip_gain: float32 [64], replicated, may hold values from 0.5 to 1.5
- filter_taps: float32 [4, 5120], replicated, may hold values from -3 to 3
- filter_bias: float32 [5120], replicated, may hold values from -3 to 3
- norm_gain: float32 [4096], replicated, may hold values from 0.5 to 1.5
Outputs:
- normed: bfloat16 [4, 16384, 4096], P('dp', 'ctx')
All inputs are finite; a program needn't handle non-finite values.
Results may differ from a plain program's by a relative error of at most 0.0061.
Values may be sent and summed in bfloat16 or wider, within the bound.
A program may use at most 192 MiB of HBM per device.

v0:
```python
import math

import jax
import jax.numpy as jnp
from jax import lax
from jax.sharding import PartitionSpec as P

HEADS = 64
HEAD_DIM = 64
STATE = 128
GROUPS = 4
BLOCK = 256
GROUP_HEADS = 16


def shifted(value, axis, steps):
    count = lax.axis_size(axis)
    initial, last = (max(0, -steps), min(count, count - steps))
    return lax.ppermute(value, axis, [(source, source + steps) for source in range(initial, last)])


def filter_rows(prefix, current, filter_taps, filter_bias):
    padded = jnp.concatenate([prefix, current], axis=0).astype(jnp.float32)
    length = current.shape[0]
    summed = filter_bias + filter_taps[0] * padded[0:length]
    for offset in range(1, filter_taps.shape[0]):
        summed = summed + filter_taps[offset] * padded[offset : offset + length]
    return summed


def ssd_group(values, input_map, output_map, step_size, decay_rate, skip_gain, block_len):
    length, head_count, head_width = values.shape
    block_count = length // block_len
    bundle = math.gcd(block_count, 8)
    bundle_count = block_count // bundle
    highest = lax.Precision.HIGHEST
    value_rows = values.reshape(block_count, block_len, head_count, head_width)
    input_rows = input_map.reshape(block_count, block_len, -1)
    output_rows = output_map.reshape(block_count, block_len, -1)
    step_rows = step_size.reshape(block_count, block_len, head_count)
    decay_sum = jnp.cumsum(-step_rows * decay_rate, axis=1)
    causal = (jnp.arange(block_len)[:, None] >= jnp.arange(block_len)[None, :])[None, :, :, None]

    def local_block(pieces):
        value_block, input_block, output_block, step_block, decay_block = pieces
        scores = jnp.einsum(
            "ktn,kun->ktu", output_block, input_block, preferred_element_type=jnp.float32
        )
        decay_gap = jnp.where(causal, decay_block[:, :, None, :] - decay_block[:, None, :, :], 0.0)
        weights = (
            jnp.where(causal, jnp.exp(decay_gap), 0.0)
            * scores[..., None]
            * step_block[:, None, :, :]
        ).astype(jnp.bfloat16)
        within = jnp.einsum(
            "ktuh,kuhp->kthp", weights, value_block, preferred_element_type=jnp.float32
        )
        to_end = jnp.exp(decay_block[:, -1:, :] - decay_block) * step_block
        scaled = (to_end[..., None] * value_block.astype(jnp.float32)).astype(jnp.bfloat16)
        states = jnp.einsum(
            "kuhp,kun->khpn", scaled, input_block, preferred_element_type=jnp.float32
        )
        return (within, states)

    def blocked(array):
        return array.reshape((bundle_count, bundle) + array.shape[1:])

    within, states = lax.map(
        local_block,
        (
            blocked(value_rows),
            blocked(input_rows),
            blocked(output_rows),
            blocked(step_rows),
            blocked(decay_sum),
        ),
    )
    within = within.reshape(block_count, block_len, head_count, head_width)
    states = states.reshape((block_count,) + states.shape[2:])
    totals = decay_sum[:, -1, :]
    running = jnp.cumsum(totals, axis=0)
    starts = running - totals
    before = (jnp.arange(block_count)[:, None] > jnp.arange(block_count)[None, :])[:, :, None]
    mixing = jnp.where(
        before, jnp.exp(jnp.where(before, starts[:, None, :] - running[None, :, :], 0.0)), 0.0
    )
    entering = jnp.einsum("kjh,jhpn->khpn", mixing, states, precision=highest)
    carried = (
        jnp.einsum("khpn,ktn->kthp", entering, output_rows.astype(jnp.float32), precision=highest)
        * jnp.exp(decay_sum)[..., None]
    )
    output = within + carried + skip_gain[:, None] * value_rows.astype(jnp.float32)
    return output.reshape(length, head_count, head_width)


def group_norm(values, norm_gain):
    length = values.shape[0]
    grouped = values.astype(jnp.float32).reshape(length, GROUPS, -1)
    mean_square = jnp.mean(jnp.square(grouped), axis=-1, keepdims=True)
    return (grouped * lax.rsqrt(mean_square + 1e-05)).reshape(length, -1) * norm_gain


def sequence_filter(projected, filter_taps, filter_bias):
    reach_rows = filter_taps.shape[0] - 1
    length = projected.shape[0]
    rim_rows = shifted(projected[length - reach_rows :], "ctx", 1)
    return jax.nn.silu(filter_rows(rim_rows, projected, filter_taps, filter_bias)).astype(
        jnp.bfloat16
    )


def head_layout(source, step_raw, step_bias, decay_rate, skip_gain):
    context_size = lax.axis_size("ctx")
    device = lax.axis_index("ctx")
    length = source.shape[0]
    inner_width = HEADS * HEAD_DIM
    local_heads = HEADS // context_size
    local_width = local_heads * HEAD_DIM
    group_share = max(1, GROUP_HEADS // local_heads)
    local_groups = max(1, local_heads // GROUP_HEADS)
    value_parts = source[:, :inner_width].reshape(length, context_size, local_width)
    map_parts = source[:, inner_width:].reshape(length, 2, GROUPS, STATE)
    map_parts = jnp.repeat(map_parts, group_share, axis=2)
    step_parts = step_raw.reshape(length, context_size, local_heads)
    moved_values, moved_input, moved_output, moved_steps = (
        lax.all_to_all(value_parts, "ctx", split_axis=1, concat_axis=0, tiled=True),
        lax.all_to_all(map_parts[:, 0], "ctx", split_axis=1, concat_axis=0, tiled=True),
        lax.all_to_all(map_parts[:, 1], "ctx", split_axis=1, concat_axis=0, tiled=True),
        lax.all_to_all(step_parts, "ctx", split_axis=1, concat_axis=0, tiled=True),
    )
    full_length = moved_values.shape[0]
    head_values = moved_values.reshape(full_length, local_width)
    input_maps = moved_input.reshape(full_length, local_groups * STATE)
    output_maps = moved_output.reshape(full_length, local_groups * STATE)
    bias_slice = lax.dynamic_slice_in_dim(step_bias, device * local_heads, local_heads, 0)
    rate_slice = lax.dynamic_slice_in_dim(decay_rate, device * local_heads, local_heads, 0)
    skip_slice = lax.dynamic_slice_in_dim(skip_gain, device * local_heads, local_heads, 0)
    step_size = jax.nn.softplus(
        moved_steps.reshape(full_length, local_heads).astype(jnp.float32) + bias_slice
    )
    inputs = head_values.reshape(full_length, local_heads, HEAD_DIM)
    pieces = ssd_group(inputs, input_maps, output_maps, step_size, rate_slice, skip_slice, BLOCK)
    mixed_rows = pieces.reshape(full_length, local_width).astype(jnp.bfloat16)
    return lax.all_to_all(mixed_rows, "ctx", split_axis=0, concat_axis=1, tiled=True)


def per_device(
    tokens,
    in_weight,
    step_weight,
    step_bias,
    decay_rate,
    skip_gain,
    filter_taps,
    filter_bias,
    norm_gain,
):
    token_rows = tokens[0]
    gathered = lax.all_gather(tokens, "dp", axis=0, tiled=True)
    partial_value = jnp.einsum(
        "btd,dc->btc", gathered, in_weight, preferred_element_type=jnp.float32
    ).astype(jnp.bfloat16)
    projected = lax.all_to_all(partial_value, "dp", split_axis=0, concat_axis=2, tiled=True)[0]
    step_raw = jnp.dot(token_rows, step_weight, preferred_element_type=jnp.float32).astype(
        jnp.bfloat16
    )
    active = sequence_filter(projected, filter_taps, filter_bias)
    mixed_rows = head_layout(active, step_raw, step_bias, decay_rate, skip_gain)
    return group_norm(mixed_rows, norm_gain).astype(jnp.bfloat16)[None]


def solution(mesh):
    in_specs = (P("dp", "ctx", None), P(None, "dp"), P(), P(), P(), P(), P(), P(), P())
    out_specs = P("dp", "ctx", None)
    return jax.shard_map(
        per_device, mesh=mesh, in_specs=in_specs, out_specs=out_specs, check_vma=False
    )
```

profile of v0, /device:TPU:24, one launch (start us, length us, event | category | flops | bytes accessed | tf_op | source)
XLA Modules:
  0.0 621.4 jit_solution(2261490554271025754)
XLA Ops:
  7.3 83.8 %all-gather.2.cloned.1.call-done = bf16[4,512,2048]{2,1,0:T(8,128)(2,1)} async-done(((bf16[1,512,2048]{2,1,0:T(8,128)(2,1)}), bf16[4,512,2048]{2,1,0:T(8,128)(2,1)}) %all-gather.2.cloned.1.call-update) | async-done | bytes 8388624 | tf_op jit(solution)/shard_map/all_gather | solution.py:159
  91.1 16.5 %convolution_convert_fusion = bf16[4,512,1280]{2,1,0:T(8,128)(2,1)} fusion(bf16[4,512,2048]{2,1,0:T(8,128)(2,1)} %all-gather.2.cloned.1.call-done, bf16[2048,1280]{1,0:T(8,128)(2,1)} %param.12), kind=kOutput, calls=%fused_computation.53 | convolution fusion | flops 10740039680 | bytes 18874368 | tf_op jit(solution)/shard_map/btd,dc->btc/dot_general | solution.py:160
  107.6 5.2 all-to-all-start
  114.2 58.0 %all-to-all-done = bf16[4,512,1280]{2,1,0:T(8,128)(2,1)} async-done(((bf16[4,512,1280]{2,1,0:T(8,128)(2,1)}), bf16[4,512,1280]{2,1,0:T(8,128)(2,1)}, u32[]{:S(2)}, u32[]{:S(2)}) %all-to-all-start) | async-done | bytes 5242912 | tf_op jit(solution)/shard_map/all_to_all | solution.py:163
  172.2 9.9 %all-to-all-start.2 = ((bf16[512,32,2]{0,2,1:T(2,128)(2,1)}), bf16[512,32,2]{0,2,1:T(2,128)(2,1)S(1)}, u32[]{:S(2)}, u32[]{:S(2)}) async-start(bf16[512,32,2]{0,2,1:T(2,128)(2,1)} %reshape.186), calls=%async_computation.2 | async-start | bytes 131072 | tf_op jit(solution)/shard_map/all_to_all | solution.py:129
  183.1 3.9 collective-permute-start
  187.1 7.9 %copy.101 = bf16[1,512,4,1280]{1,3,2,0:T(8,128)(2,1)} copy(bf16[1,512,4,1280]{3,1,2,0:T(8,128)(2,1)} %bitcast.3) | data formatting | bytes 10485760 | tf_op jit(solution)/shard_map/all_to_all | solution.py:163
  195.0 1.6 copy.102
  196.5 5.8 maximum_convert_fusion
  202.4 13.7 %multiply_convert_fusion.8 = bf16[512,5120]{0,1:T(8,128)(2,1)S(1)} fusion(f32[515,5120]{0,1:T(8,128)S(1)} %maximum_convert_fusion, f32[5120]{0:T(1024)S(1)} %bitcast.211, f32[5120]{0:T(1024)S(1)} %bitcast.212, f32[5120]{0:T(1024)S(1)} %bitcast.210, f32[5120]{0:T(1024)S(1)} %bitcast.209, f32[5120]{0:T(1024)S(1)} %copy-done.5), kind=kLoop, calls=%fused_computation.43 | loop fusion | flops 34078720 | bytes 47288320 | tf_op jit(solution)/shard_map/convert_element_type | solution.py:107
  216.1 2.3 copy-done.2
  219.1 2.0 broadcast_in_dim.79
  221.1 3.7 slice_bitcast_fusion.1
  224.8 9.6 %all-to-all-start.3 = ((bf16[512,32,128]{2,0,1:T(8,128)(2,1)}), bf16[512,32,128]{2,0,1:T(8,128)(2,1)}, u32[]{:S(2)}, u32[]{:S(2)}) async-start(bf16[512,32,128]{2,0,1:T(8,128)(2,1)} %get-tuple-element.157), calls=%async_computation.3 | async-start | bytes 8388608 | tf_op jit(solution)/shard_map/all_to_all | solution.py:128
  234.4 4.5 slice.79
  238.9 46.2 %all-to-all-done.3 = bf16[512,32,128]{2,0,1:T(8,128)(2,1)} async-done(((bf16[512,32,128]{2,0,1:T(8,128)(2,1)}), bf16[512,32,128]{2,0,1:T(8,128)(2,1)}, u32[]{:S(2)}, u32[]{:S(2)}) %all-to-all-start.3) | async-done | bytes 4194336 | tf_op jit(solution)/shard_map/all_to_all | solution.py:128
  285.1 63.5 %all_to_all.79 = bf16[512,32,128]{0,2,1:T(8,128)(2,1)} all-to-all(bf16[512,32,128]{0,2,1:T(8,128)(2,1)} %bitcast.202), channel_id=1, replica_groups=mesh['dp'=4,'ctx'=32] {'ctx'}, dimensions={1} | all-to-all | bytes 8388608 | tf_op jit(solution)/shard_map/all_to_all | solution.py:126
  348.6 6.8 %all-to-all-start.4 = ((bf16[512,32,128]{2,0,1:T(8,128)(2,1)}), bf16[512,32,128]{2,0,1:T(8,128)(2,1)}, u32[]{:S(2)}, u32[]{:S(2)}) async-start(bf16[512,32,128]{2,0,1:T(8,128)(2,1)} %get-tuple-element.156), calls=%async_computation.4 | async-start | bytes 8388608 | tf_op jit(solution)/shard_map/all_to_all | solution.py:127
  356.0 1.2 reduce-window.6
  359.4 6.4 %copy.103 = bf16[32,512,1,128]{1,0,3,2:T(8,128)(2,1)} copy(bf16[32,512,1,128]{1,3,0,2:T(8,128)(2,1)} %bitcast.197) | data formatting | bytes 8388608 | tf_op jit(solution)/shard_map/all_to_all | solution.py:126
  365.9 7.1 %reshape_reshape_reshape_reshape.3 = bf16[8,8,256,2,64]{2,1,0,4,3:T(8,128)(2,1)} reshape(bf16[32,512,1,128]{1,0,3,2:T(8,128)(2,1)} %copy.103) | data formatting | bytes 8388608 | tf_op jit(solution)/shard_map/reshape;reshape;reshape;reshape | solution.py:66
  373.0 32.9 %all-to-all-done.4 = bf16[512,32,128]{2,0,1:T(8,128)(2,1)} async-done(((bf16[512,32,128]{2,0,1:T(8,128)(2,1)}), bf16[512,32,128]{2,0,1:T(8,128)(2,1)}, u32[]{:S(2)}, u32[]{:S(2)}) %all-to-all-start.4) | async-done | bytes 4194336 | tf_op jit(solution)/shard_map/all_to_all | solution.py:127
  405.9 64.5 %while.14 = (s32[]{:T(128)}, f32[8,8,256,2,64]{2,4,3,1,0:T(8,128)}, f32[8,8,2,64,128]{4,3,2,1,0:T(8,128)}, bf16[8,8,256,2,64]{2,1,0,4,3:T(8,128)(2,1)}, f32[8,8,...) while((s32[]{:T(128)}, f32[8,8,256,2,64]{2,4,3,1,0:T(8,128)}, ...), condition=%wide.region_3.4_spmd.clone.clone, body=%wide.region_2.3_spmd.clone.clone.sunk | while | flops 342695936 | bytes 9915173 | solution.py:68
  405.9 1.6 fusion.76
  407.5 1.1 constant_dynamic-slice_fusion.6
  408.6 2.5 fusion.78
  411.8 2.1 fusion.79
  413.9 1.6 fusion.76
  415.6 1.1 constant_dynamic-slice_fusion.6
  416.7 2.5 fusion.78
  419.8 2.1 fusion.79
  422.0 1.6 fusion.76
  423.6 1.1 constant_dynamic-slice_fusion.6
  424.7 2.5 fusion.78
  427.9 2.1 fusion.79
  430.0 1.6 fusion.76
  431.7 1.1 constant_dynamic-slice_fusion.6
  432.8 2.5 fusion.78
  435.9 2.1 fusion.79
  438.1 1.6 fusion.76
  439.7 1.1 constant_dynamic-slice_fusion.6
  440.8 2.5 fusion.78
  444.0 2.1 fusion.79
  446.1 1.6 fusion.76
  448.9 2.5 fusion.78
  452.0 2.1 fusion.79
  454.2 1.6 fusion.76
  456.9 2.5 fusion.78
  460.1 2.1 fusion.79
  462.2 1.6 fusion.76
  465.0 2.5 fusion.78
  468.2 2.1 fusion.79
  470.3 3.4 bitcast_convert_fusion
  473.7 8.1 %copy.121 = f32[32,512,1,128]{1,0,3,2:T(8,128)} copy(f32[32,512,1,128]{1,3,0,2:T(8,128)S(1)} %bitcast_convert_fusion) | data formatting | bytes 16777216 | tf_op jit(solution)/shard_map/convert_element_type | solution.py:92
  481.8 9.5 %reshape.196 = f32[64,256,2,64]{1,0,3,2:T(8,128)} reshape(f32[32,512,1,128]{1,0,3,2:T(8,128)} %copy.121) | data formatting | bytes 16777216 | tf_op jit(solution)/shard_map/convert_element_type | solution.py:92
  491.3 10.4 %fusion.39 = f32[64,2,64,128]{3,0,2,1:T(8,128)} fusion(f32[64,2,64,128]{3,2,1,0:T(8,128)} %bitcast.204, f32[64,2]{0,1:T(2,128)S(1)} %copy.117, f32[64,2]{0,1:T(2,128)S(1)} %subtract_reduce_fusion, pred[64,64]{1,0:T(8,128)(4,1)S(1)} %iota_compare_fusion.1), kind=kOutput, calls=%fused_computation.61 | convolution fusion | flops 805330944 | bytes 8393728 | tf_op jit(solution)/shard_map/kjh,jhpn->khpn/dot_general | solution.py:87
  501.7 20.7 %fusion.31 = bf16[64,256,2,64]{1,3,2,0:T(8,128)(2,1)} fusion(f32[8,8,256,2,64]{2,4,3,1,0:T(8,128)} %get-tuple-element.56, f32[64,256,2,64]{1,0,3,2:T(8,128)} %reshape.196, f32[2]{0:T(128)S(1)} %dynamic_slice.29, f32[64,256,2]{1,2,0:T(2,128)S(1)} %copy.120, bf16[64,256,128,1]{2,1,3,0:T(8,128)(2,1)} %bitcast.35, f32[64,2,64,128]{3,0,2,1:T(8,128)} %fusion.39), kind=kOutput, calls=%fused_computation.49 | convolution fusion | flops 3231711232 | bytes 29491208 | tf_op jit(solution)/shard_map/khpn,ktn->kthp/dot_general | solution.py:89
  522.4 6.5 %copy.123 = bf16[64,256,2,64]{1,0,3,2:T(8,128)(2,1)} copy(bf16[64,256,2,64]{1,3,2,0:T(8,128)(2,1)} %fusion.31) | data formatting | bytes 8388608 | tf_op jit(solution)/shard_map/convert_element_type | solution.py:143
  528.9 7.1 %convert_element_type.101 = bf16[32,512,128]{1,0,2:T(8,128)(2,1)} reshape(bf16[64,256,2,64]{1,0,3,2:T(8,128)(2,1)} %copy.123) | data formatting | bytes 8388608 | tf_op jit(solution)/shard_map/convert_element_type | solution.py:143
  536.0 4.5 copy.124
  540.5 62.9 %all_to_all.80 = bf16[32,512,128]{1,2,0:T(8,128)(2,1)S(1)} all-to-all(bf16[32,512,128]{1,2,0:T(8,128)(2,1)S(1)} %copy.124), channel_id=1, replica_groups=mesh['dp'=4,'ctx'=32] {'ctx'}, dimensions={0} | all-to-all | bytes 8388608 | tf_op jit(solution)/shard_map/all_to_all | solution.py:144
  604.4 1.1 convert_element_type.116
  605.6 2.4 fusion.29
  608.0 6.3 %copy.125 = bf16[1,512,4096]{2,1,0:T(8,128)(2,1)} copy(bf16[1,512,4096]{1,2,0:T(8,128)(2,1)} %fusion.29) | data formatting | bytes 8388608 | tf_op jit(solution)/shard_map/convert_element_type | solution.py:169
  (133 shorter events, 16.0 us)
Async XLA Ops:
  6.5 106.2 %copy-start = (bf16[2048,64]{0,1:T(8,128)(2,1)S(1)}, bf16[2048,64]{0,1:T(8,128)(2,1)}, u32[]{:S(2)}) copy-start(bf16[2048,64]{0,1:T(8,128)(2,1)} %param.13) | copy-start | bytes 786436
  6.5 84.6 %all-gather.2.cloned.1.call-start = ((), (), s32[]{:S(2)}) async-start(), calls=%async_computation.6 | async-start | bytes 10485760 | tf_op jit(solution)/shard_map/all_gather | solution.py:159
  107.6 5.2 copy-start.3
  107.6 79.4 %copy-start.4 = (f32[4,5120]{1,0:T(4,128)S(1)}, f32[4,5120]{1,0:T(4,128)}, u32[]{:S(2)}) copy-start(f32[4,5120]{1,0:T(4,128)} %param.17) | copy-start | bytes 245764
  107.6 64.7 %all-to-all-start = ((bf16[4,512,1280]{2,1,0:T(8,128)(2,1)}), bf16[4,512,1280]{2,1,0:T(8,128)(2,1)}, u32[]{:S(2)}, u32[]{:S(2)}) async-start(bf16[4,512,1280]{2,1,0:T(8,128)(2,1)} %convolution_convert_fusion), calls=%async_computation | async-start | bytes 10485760 | tf_op jit(solution)/shard_map/all_to_all | solution.py:163
  172.2 52.6 %all-to-all-start.2 = ((bf16[512,32,2]{0,2,1:T(2,128)(2,1)}), bf16[512,32,2]{0,2,1:T(2,128)(2,1)S(1)}, u32[]{:S(2)}, u32[]{:S(2)}) async-start(bf16[512,32,2]{0,2,1:T(2,128)(2,1)} %reshape.186), calls=%async_computation.2 | async-start | bytes 131072 | tf_op jit(solution)/shard_map/all_to_all | solution.py:129
  183.1 11.9 %collective-permute-start = (bf16[3,5120]{1,0:T(4,128)(2,1)S(1)}, bf16[3,5120]{1,0:T(4,128)(2,1)S(1)}, u32[]{:S(2)}, u32[]{:S(2)}) collective-permute-start(bf16[3,5120]{1,0:T(4,128)(2,1)S(1)} %bitcast.213), channel_id=1, source_target_pairs={{0,1},{1,2},{2,3},{3,4},{4,5},{5,6},{6,7},{7,8},{8,9},{9,10},{10,1... | collective-permute-start | bytes 92168 | tf_op jit(solution)/shard_map/ppermute | solution.py:19
  196.5 5.8 copy-start.5
  216.1 2.3 copy-start.2
  224.8 60.3 %all-to-all-start.3 = ((bf16[512,32,128]{2,0,1:T(8,128)(2,1)}), bf16[512,32,128]{2,0,1:T(8,128)(2,1)}, u32[]{:S(2)}, u32[]{:S(2)}) async-start(bf16[512,32,128]{2,0,1:T(8,128)(2,1)} %get-tuple-element.157), calls=%async_computation.3 | async-start | bytes 8388608 | tf_op jit(solution)/shard_map/all_to_all | solution.py:128
  348.5 6.9 %copy-start.7 = (f32[64]{0:T(128)S(1)}, f32[64]{0:T(128)}, u32[]{:S(2)}) copy-start(f32[64]{0:T(128)} %param.14) | copy-start | bytes 772
  348.5 7.0 %copy-start.8 = (f32[64]{0:T(128)S(1)}, f32[64]{0:T(128)}, u32[]{:S(2)}) copy-start(f32[64]{0:T(128)} %param.15) | copy-start | bytes 772
  348.6 7.0 %copy-start.9 = (f32[64]{0:T(128)S(1)}, f32[64]{0:T(128)}, u32[]{:S(2)}) copy-start(f32[64]{0:T(128)} %param.16) | copy-start | bytes 772
  348.6 57.3 %all-to-all-start.4 = ((bf16[512,32,128]{2,0,1:T(8,128)(2,1)}), bf16[512,32,128]{2,0,1:T(8,128)(2,1)}, u32[]{:S(2)}, u32[]{:S(2)}) async-start(bf16[512,32,128]{2,0,1:T(8,128)(2,1)} %get-tuple-element.156), calls=%async_computation.4 | async-start | bytes 8388608 | tf_op jit(solution)/shard_map/all_to_all | solution.py:127
  604.4 1.2 copy-start.6
  605.6 8.8 %copy-start.1 = (bf16[2048,64]{0,1:T(8,128)(2,1)S(1)}, bf16[2048,64]{0,1:T(8,128)(2,1)}, u32[]{:S(2)}) copy-start(bf16[2048,64]{0,1:T(8,128)(2,1)} %param.13) | copy-start | bytes 786436
Sparse Core Ops, SparseCore 0:
  9.0 82.0 all-gather.1
where the time goes:
time: 633 us; the launch traced here: 621 us
  waiting for transfers between devices  222 us (35%)
  blocking collectives  126 us (20%)
  matrix products  98.5 us (16%)
  local copies, waits for them, and re-layouts  93.8 us (15%)
  starting transfers between devices  35.5 us (6%)
  other arithmetic  31.2 us (5%)
  between operations  13.9 us (2%)
    all_gather x1, waiting for transfers between devices, per_device(): gathered = lax.all_gather(tokens, 'dp', axis=0, tiled=True)  83.8 us
    all_to_all x1, blocking collectives, head_layout(): lax.all_to_all(value_parts, 'ctx', split_axis=1, concat_axis=0, tiled=True)  63.5 us
    all_to_all x1, blocking collectives, head_layout(): lax.all_to_all(mixed_rows, 'ctx', split_axis=0, concat_axis=1, tiled=True)  62.9 us
    all_to_all x1, waiting for transfers between devices, per_device(): lax.all_to_all(partial_value, 'dp', split_axis=0, concat_axis=2, tiled=True)  58 us
    all_to_all x1, waiting for transfers between devices, head_layout(): lax.all_to_all(map_parts[:, 1], 'ctx', split_axis=1, concat_axis=0, tiled...  46.2 us
    all_to_all x1, waiting for transfers between devices, head_layout(): lax.all_to_all(map_parts[:, 0], 'ctx', split_axis=1, concat_axis=0, tiled...  32.9 us
    dot_general x1, matrix products, ssd_group(): jnp.einsum('khpn,ktn->kthp', entering, output_rows.astype(jnp.float32), p...  20.7 us
    dot_general x8, matrix products, local_block(): jnp.einsum('ktuh,kuhp->kthp', weights, value_block, preferred_element_typ...  20 us
  transfers between devices with their start and end apart: 6, of which 4 were waited for; matrix products, arithmetic and copies ran while one was open for 10% of the time, Pallas kernels for 0%

commit v1 on v0

v1 whole, which is shorter than its diff:
```python
import functools

import jax
import jax.numpy as jnp
from jax import lax
from jax.experimental import pallas as pl
from jax.experimental.pallas import tpu as pltpu
from jax.sharding import PartitionSpec as P

D = 2048
HEADS = 64
HEAD_DIM = 64
STATE = 128
GROUPS = 4
BLOCK = 256
ROWS = 512
HALO = 16
SHARD = 1280
XBC = 5120
INNER = 4096
LOG2E = 1.4426950408889634
MESH = pl.DeviceIdType.MESH
F32 = jnp.float32
BF16 = jnp.bfloat16

RING_COL = ((0, 4, 1, 5), (2, 6, 3, 7))
SAME_SLOT = (10, 11, 14, 15, 16)
OTHER_SLOT = (12, 13, 17, 18, 19)


def same_slot(column):
    return 2 * SAME_SLOT[column // 2] + column % 2


def other_slot(column):
    return 2 * OTHER_SLOT[column // 2] + column % 2


def project_kernel(
    tok_ref, w_ref, sw_ref, small_ref, taps_ref, fb_ref,
    act_ref, a_ref, bt_ref, lt_ref, w2_ref, e2_ref, misc_ref,
    tok, wbuf, pbuf, abuf, swp,
    loc_sem, tok_sem, act_sem, halo_sem, sib_send, sib_recv,
    x_send, x_recv, ring_send, ring_recv, fwd_send, fwd_recv,
):
    dp = lax.axis_index("dp")
    ctx = lax.axis_index("ctx")
    z = ctx % 4
    y = (ctx // 4) % 4
    xh = ctx // 16
    sibling = dp + 1 - 2 * (dp % 2)
    across = (dp + 2) % 4
    place = (z, y)

    def along(dim, step):
        if dim == 0:
            return xh * 16 + y * 4 + (z + step) % 4
        return xh * 16 + ((y + step) % 4) * 4 + z

    source_a = (across, ctx)
    source_b = (across, (ctx + 16) % 32)
    after = (dp, (ctx + 1) % 32)
    before = (dp, (ctx + 31) % 32)

    tok_copy = pltpu.make_async_copy(tok_ref.at[0], tok.at[HALO:], tok_sem)
    tok_copy.start()

    def loc_copy(j):
        return pltpu.make_async_copy(
            w_ref.at[:, j * 128 : (j + 1) * 128], wbuf.at[j], loc_sem.at[j]
        )

    barrier = pltpu.get_barrier_semaphore()
    for peer in (
        (sibling, ctx), source_a, source_b, after, before,
        (dp, along(0, 1)), (dp, along(0, 3)), (dp, along(1, 1)), (dp, along(1, 3)),
    ):
        pl.semaphore_signal(barrier, inc=1, device_id=peer, device_id_type=MESH)
    for j in range(4):
        loc_copy(j).start()
    pl.semaphore_wait(barrier, 9)

    def remote(src, dst, send, recv, peer):
        return pltpu.make_async_remote_copy(
            src_ref=src, dst_ref=dst, send_sem=send, recv_sem=recv,
            device_id=peer, device_id_type=MESH,
        )

    def x_piece(dim, p):
        column = RING_COL[dim][p]
        rows = pl.ds(pl.multiple_of(place[dim] * 512, 512), 512)
        peer = source_a if p < 2 else source_b
        return remote(
            w_ref.at[rows, column * 128 : (column + 1) * 128],
            wbuf.at[same_slot(column), rows],
            x_send.at[dim * 4 + p], x_recv.at[dim * 4 + p], peer,
        )

    def x_direct(k):
        column = 8 + k
        return remote(
            w_ref.at[:, column * 128 : (column + 1) * 128],
            wbuf.at[same_slot(column)],
            x_send.at[8 + k], x_recv.at[8 + k], (source_a, source_b)[k],
        )

    def ring_rows(dim, kind, p):
        back = (3, 1, 2)[kind]
        return pl.ds(pl.multiple_of(((place[dim] + back) % 4) * 512, 512), 512)

    def ring_out(dim, kind, p):
        column = RING_COL[dim][p]
        if kind == 0:
            rows, peer = pl.ds(pl.multiple_of(place[dim] * 512, 512), 512), along(dim, 1)
        elif kind == 1:
            rows, peer = pl.ds(pl.multiple_of(place[dim] * 512, 512), 512), along(dim, 3)
        elif p < 2:
            rows, peer = ring_rows(dim, 0, p), along(dim, 1)
        else:
            rows, peer = ring_rows(dim, 1, p), along(dim, 3)
        at = wbuf.at[same_slot(column), rows]
        index = dim * 12 + kind * 4 + p
        return remote(at, at, ring_send.at[index], ring_recv.at[index], (dp, peer))

    def ring_in(dim, kind, p):
        column = RING_COL[dim][p]
        at = wbuf.at[same_slot(column), ring_rows(dim, kind, p)]
        index = dim * 12 + kind * 4 + p
        return remote(at, at, ring_send.at[index], ring_recv.at[index], (dp, along(dim, 1)))

    def forward(index):
        if index in (8, 9):
            src, dst = wbuf.at[same_slot(index)], wbuf.at[other_slot(index)]
        else:
            if index < 8:
                dim, p = divmod(index, 4)
                rows = pl.ds(pl.multiple_of(place[dim] * 512, 512), 512)
            else:
                dim, rest = divmod(index - 10, 12)
                kind, p = divmod(rest, 4)
                rows = ring_rows(dim, kind, p)
            column = RING_COL[dim][p]
            src = wbuf.at[same_slot(column), rows]
            dst = wbuf.at[other_slot(column), rows]
        return remote(src, dst, fwd_send.at[index], fwd_recv.at[index], (sibling, ctx))

    def sib_copy(j):
        return remote(
            w_ref.at[:, j * 128 : (j + 1) * 128], wbuf.at[10 + j],
            sib_send.at[j], sib_recv.at[j], (sibling, ctx),
        )

    halo_copy = remote(
        tok_ref.at[0, ROWS - HALO :], tok.at[:HALO], halo_sem.at[0], halo_sem.at[1], after
    )
    halo_copy.start()
    for p, q in ((0, 2), (1, 3)):
        x_piece(0, p).start()
        x_piece(1, q).start()
        x_piece(1, p).start()
        x_piece(0, q).start()
    x_direct(0).start()
    x_direct(1).start()
    for j in range(4, 10):
        loc_copy(j).start()
    for j in range(10):
        sib_copy(j).start()

    swp[...] = jnp.zeros_like(swp)
    swp[:, 0:HEADS] = sw_ref[...]
    tok_copy.wait()
    step_raw = jnp.dot(tok[HALO:], swp[...], preferred_element_type=F32)
    step_raw = step_raw.astype(BF16).astype(F32) + small_ref[0:1]
    step = jnp.maximum(step_raw, 0.0) + jnp.log1p(jnp.exp(-jnp.abs(step_raw)))
    keep = lax.broadcasted_iota(jnp.int32, (ROWS, 128), 1) < HEADS
    step = jnp.where(keep, step, 0.0)
    fall = step * (small_ref[1:2] * (-LOG2E))
    lower = (
        lax.broadcasted_iota(jnp.int32, (BLOCK, BLOCK), 0)
        >= lax.broadcasted_iota(jnp.int32, (BLOCK, BLOCK), 1)
    ).astype(F32)
    level = jnp.log2(step)

    def halves(value):
        high = value.astype(BF16).astype(F32)
        low = (value - high).astype(BF16).astype(F32)
        return (high + pltpu.roll(low, 64, 1)).astype(BF16)

    ends = []
    for k in range(2):
        at = slice(k * BLOCK, (k + 1) * BLOCK)
        a = jnp.dot(
            lower, fall[at], precision=lax.Precision.HIGHEST, preferred_element_type=F32
        )
        end = a[BLOCK - 1 : BLOCK]
        ends.append(end)
        weight = jnp.where(keep[at], jnp.exp2(end - a) * step[at], 0.0)
        w2_ref[at] = halves(weight)
        e2_ref[at] = halves(jnp.where(keep[at], jnp.exp2(a), 0.0))
        for g in range(GROUPS):
            a_ref[g, at] = a if g == 0 else pltpu.roll(a, 128 - 16 * g, 1)
        bt_ref[:, at] = jnp.transpose(level[at] - a)
        lt_ref[:, at] = jnp.transpose(level[at])
    row = lax.broadcasted_iota(jnp.int32, (8, 128), 0)
    lane_ok = lax.broadcasted_iota(jnp.int32, (8, 128), 1) < HEADS
    exponent = jnp.where(row == 0, ends[0], jnp.where(row == 1, ends[1], ends[0] + ends[1]))
    rows_of = jnp.where(row == 3, small_ref[2:3], jnp.exp2(exponent))
    misc_ref[...] = halves(jnp.where(lane_ok, rows_of, 0.0))

    halo_copy.wait_recv()

    @pl.when(ctx == 0)
    def _():
        tok[:HALO] = jnp.zeros((HALO, D), BF16)

    def x_arrive(dim, p):
        x_piece(dim, p).wait_recv()
        ring_out(dim, 0, p).start()
        ring_out(dim, 1, p).start()
        forward(dim * 4 + p).start()

    def near_arrive(dim, kind, p):
        ring_in(dim, kind, p).wait_recv()
        if (kind == 0) == (p < 2):
            ring_out(dim, 2, p).start()
        forward(10 + dim * 12 + kind * 4 + p).start()

    def far_arrive(dim, p):
        ring_in(dim, 2, p).wait_recv()
        forward(10 + dim * 12 + 8 + p).start()

    def direct_arrive(k):
        x_direct(k).wait_recv()
        forward(8 + k).start()

    def other_wait(pieces):
        for dim, p in pieces:
            forward(dim * 4 + p).wait_recv()
            for kind in range(3):
                forward(10 + dim * 12 + kind * 4 + p).wait_recv()

    first = ((0, 0), (1, 2), (1, 0), (0, 2))
    second = ((0, 1), (1, 3), (1, 1), (0, 3))

    def events(i):
        for j in range(5):
            @pl.when(i == j)
            def _(j=j):
                loc_copy(2 * j).wait()
                loc_copy(2 * j + 1).wait()

            @pl.when(i == 5 + j)
            def _(j=j):
                sib_copy(2 * j).wait_recv()
                sib_copy(2 * j + 1).wait_recv()

        @pl.when(i == 2)
        def _():
            x_arrive(*first[0])
            x_arrive(*first[1])

        @pl.when(i == 5)
        def _():
            x_arrive(*first[2])
            x_arrive(*first[3])

        @pl.when(i == 7)
        def _():
            for piece in first[:2]:
                near_arrive(piece[0], 0, piece[1])
                near_arrive(piece[0], 1, piece[1])
            x_arrive(*second[0])
            x_arrive(*second[1])

        @pl.when(i == 9)
        def _():
            for piece in first[2:]:
                near_arrive(piece[0], 0, piece[1])
                near_arrive(piece[0], 1, piece[1])
            x_arrive(*second[2])
            x_arrive(*second[3])

        @pl.when(i == 10)
        def _():
            for piece in first:
                far_arrive(*piece)

        @pl.when(i == 11)
        def _():
            for piece in second[:2]:
                near_arrive(piece[0], 0, piece[1])
                near_arrive(piece[0], 1, piece[1])

        @pl.when(i == 12)
        def _():
            other_wait(((0, 0), (0, 2)))

        @pl.when(i == 13)
        def _():
            other_wait(((1, 0), (1, 2)))
            for piece in second[2:]:
                near_arrive(piece[0], 0, piece[1])
                near_arrive(piece[0], 1, piece[1])

        @pl.when(i == 14)
        def _():
            for piece in second:
                far_arrive(*piece)

        @pl.when(i == 15)
        def _():
            direct_arrive(0)
            direct_arrive(1)

        @pl.when(i == 17)
        def _():
            other_wait(((0, 1), (0, 3)))

        @pl.when(i == 18)
        def _():
            other_wait(((1, 1), (1, 3)))

        @pl.when(i == 19)
        def _():
            forward(8).wait_recv()
            forward(9).wait_recv()

    def column_of(i):
        m = i - 10
        foreign = i // 10
        late = (i - 6) // 8 * foreign
        kind = foreign * (2 + (1 - late) * ((m % 4) // 2) + late * ((i - 14 + 30) // 3 - 10))
        near_kind = (1 - foreign) * (i // 5)
        pair = (1 - foreign) * (i % 5) + foreign * (
            (1 - late) * (m % 2) + late * (2 + (i - 14 + 30) % 3)
        )
        relation = kind + near_kind
        lo = (dp + relation) % 2
        hi = (dp // 2 + relation // 2) % 2
        return (2 * hi + lo) * SHARD + pair * 256

    def act_copy(i):
        columns = pl.ds(pl.multiple_of(column_of(i), 256), 256)
        return pltpu.make_async_copy(abuf.at[i], act_ref.at[:, columns], act_sem)

    @pl.loop(0, 20)
    def _(i):
        events(i)
        weights = jnp.concatenate([wbuf[2 * i], wbuf[2 * i + 1]], axis=1)
        pbuf[...] = (
            jnp.dot(tok[...], weights, preferred_element_type=F32).astype(BF16).astype(F32)
        )
        columns = pl.ds(pl.multiple_of(column_of(i), 256), 256)
        taps = taps_ref[:, columns]
        summed = fb_ref[:, columns] + taps[0:1] * pbuf[HALO - 3 : HALO - 3 + ROWS]
        for k in range(1, 4):
            summed = summed + taps[k : k + 1] * pbuf[HALO - 3 + k : HALO - 3 + k + ROWS]
        abuf[i] = (summed / (1.0 + jnp.exp(-summed))).astype(BF16)
        act_copy(i).start()

    halo_copy.wait_send()
    for dim in range(2):
        for p in range(4):
            x_piece(dim, p).wait_send()
            for kind in range(3):
                ring_out(dim, kind, p).wait_send()
    for k in range(2):
        x_direct(k).wait_send()
    for j in range(10):
        sib_copy(j).wait_send()
    for index in range(34):
        forward(index).wait_send()
    pltpu.make_async_copy(abuf, abuf, act_sem).wait()


def project(tokens, in_weight, step_weight, small, filter_taps, filter_bias):
    vmem = pl.BlockSpec(memory_space=pltpu.VMEM)
    anywhere = pl.BlockSpec(memory_space=pl.ANY)
    dma = pltpu.SemaphoreType.DMA
    return pl.pallas_call(
        project_kernel,
        out_shape=(
            jax.ShapeDtypeStruct((ROWS, XBC), BF16),
            jax.ShapeDtypeStruct((GROUPS, ROWS, 128), F32),
            jax.ShapeDtypeStruct((128, ROWS), F32),
            jax.ShapeDtypeStruct((128, ROWS), F32),
            jax.ShapeDtypeStruct((ROWS, 128), BF16),
            jax.ShapeDtypeStruct((ROWS, 128), BF16),
            jax.ShapeDtypeStruct((8, 128), BF16),
        ),
        in_specs=[anywhere, anywhere, vmem, vmem, vmem, vmem],
        out_specs=(anywhere,) + (vmem,) * 6,
        scratch_shapes=[
            pltpu.VMEM((HALO + ROWS, D), BF16),
            pltpu.VMEM((40, D, 128), BF16),
            pltpu.VMEM((HALO + ROWS, 256), F32),
            pltpu.VMEM((20, ROWS, 256), BF16),
            pltpu.VMEM((D, 128), BF16),
            dma((10,)), dma, dma, dma((2,)), dma((10,)), dma((10,)),
            dma((10,)), dma((10,)), dma((24,)), dma((24,)), dma((34,)), dma((34,)),
        ],
        compiler_params=pltpu.CompilerParams(
            collective_id=0, has_side_effects=True, vmem_limit_bytes=56 * 2**20
        ),
        name="project",
    )(tokens, in_weight, step_weight, small, filter_taps, filter_bias)


def mix_kernel(
    act_ref, a_ref, bt_ref, lt_ref, w2_ref, e2_ref, misc_ref, gain_ref,
    out_ref,
    spread, first, mix, scores, state_out, decay_out, state_in, decay_in, enter_out, enter_in,
    sems,
):
    dp = lax.axis_index("dp")
    me = lax.axis_index("ctx")
    barrier = pltpu.get_barrier_semaphore()

    @pl.loop(1, 32)
    def _(r):
        pl.semaphore_signal(
            barrier, inc=1, device_id=(dp, (me + r) % 32), device_id_type=MESH
        )

    head_row = lax.broadcasted_iota(jnp.int32, (128, 1024), 0) % HEADS
    head_lane = lax.broadcasted_iota(jnp.int32, (128, 1024), 1) // HEAD_DIM
    for g in range(GROUPS):
        spread[g] = (head_row == head_lane + 16 * g).astype(F32).astype(BF16)

    def widen(value, g):
        return jnp.dot(value, spread[g], preferred_element_type=F32)

    def columns(start, size):
        return pl.ds(pl.multiple_of(start, 128), size)

    @pl.loop(0, GROUPS)
    def _(g):
        decays = widen(misc_ref[...], g)
        total = None
        for k in range(2):
            at = slice(k * BLOCK, (k + 1) * BLOCK)
            values = act_ref[at, columns(g * 1024, 1024)].astype(F32)
            scaled = (widen(w2_ref[at], g) * values).astype(BF16)
            maps = act_ref[at, columns(INNER + g * STATE, STATE)]
            state = lax.dot_general(
                maps, scaled, (((0,), (0,)), ((), ())), preferred_element_type=F32
            )
            if k == 0:
                first[g] = state
                total = decays[1:2] * state
            else:
                total = total + state
        for i in range(8):
            lanes = slice(i * 128, (i + 1) * 128)
            state_out[g * 8 + i] = total[:, lanes].astype(BF16)
            decay_out[g * 8 + i] = jnp.broadcast_to(decays[2:3, lanes], (8, 128))

    def send(r, src, dst, pair):
        peer = (me + r) % 32
        return pltpu.make_async_remote_copy(
            src_ref=src.at[peer], dst_ref=dst.at[me],
            send_sem=sems.at[pair], recv_sem=sems.at[pair + 1],
            device_id=(dp, peer), device_id_type=MESH,
        )

    def wait_all(buffer, index):
        part = buffer.at[0:31]
        pltpu.make_async_copy(part, part, sems.at[index]).wait()

    pl.semaphore_wait(barrier, 31)

    @pl.loop(1, 32)
    def _(r):
        send(r, decay_out, decay_in, 2).start()
        send(r, state_out, state_in, 0).start()

    state_in[me] = state_out[me]
    decay_in[me] = decay_out[me]

    lane = lax.broadcasted_iota(jnp.int32, (BLOCK, 128), 1) < HEAD_DIM
    causal = lax.broadcasted_iota(jnp.int32, (128, 128), 0) >= lax.broadcasted_iota(
        jnp.int32, (128, 128), 1
    )

    def within(n):
        g = n // 2
        start = (n % 2) * BLOCK
        rows = pl.ds(pl.multiple_of(start, BLOCK), BLOCK)
        read = act_ref[rows, columns(INNER + GROUPS * STATE + g * STATE, STATE)]
        write = act_ref[rows, columns(INNER + g * STATE, STATE)]
        full = lax.dot_general(
            read, write, (((1,), (1,)), ((), ())), preferred_element_type=F32
        )
        scores[0] = jnp.where(causal, full[:128, :128], 0.0)
        scores[1] = full[128:, :128]
        scores[2] = jnp.where(causal, full[128:, 128:], 0.0)
        skip = widen(misc_ref[...], g)[3:4]
        for i in range(8):
            lanes = columns(g * 1024 + i * 128, 128)
            values = act_ref[rows, lanes]
            made = []
            for h in (2 * i, 2 * i + 1):
                upper = a_ref[g, pl.ds(pl.multiple_of(start, BLOCK), 128), h : h + 1]
                under = a_ref[g, pl.ds(pl.multiple_of(start + 128, 128), 128), h : h + 1]
                b0 = bt_ref[g, h : h + 1, columns(start, 128)]
                b1 = bt_ref[g, h : h + 1, columns(start + 128, 128)]
                l0 = lt_ref[g, h : h + 1, columns(start, 128)]
                l1 = lt_ref[g, h : h + 1, columns(start + 128, 128)]
                w00 = (jnp.exp2(jnp.minimum(upper + b0, l0)) * scores[0]).astype(BF16)
                w10 = (jnp.exp2(under + b0) * scores[1]).astype(BF16)
                w11 = (jnp.exp2(jnp.minimum(under + b1, l1)) * scores[2]).astype(BF16)
                top = jnp.dot(w00, values[:128], preferred_element_type=F32)
                low = jnp.dot(
                    jnp.concatenate([w10, w11], axis=1), values, preferred_element_type=F32
                )
                made.append(jnp.concatenate([top, low], axis=0))
            mixed = jnp.where(lane, made[0], made[1])
            mix[rows, lanes] = mixed + skip[:, i * 128 : (i + 1) * 128] * values.astype(F32)

    pl.loop(0, 4)(within)

    wait_all(decay_in, 3)
    wait_all(state_in, 1)

    def scan(k, carry):
        enter_out[k] = carry.astype(BF16)
        return decay_in[k, 0:1] * carry + state_in[k].astype(F32)

    lax.fori_loop(0, 32, scan, jnp.zeros((STATE, 128), F32))

    @pl.loop(1, 32)
    def _(r):
        send(r, enter_out, enter_in, 4).start()

    enter_in[me] = enter_out[me]

    pl.loop(4, 8)(within)

    wait_all(enter_in, 5)

    @pl.loop(0, GROUPS)
    def _(g):
        decays = widen(misc_ref[...], g)
        enter = jnp.concatenate([enter_in[g * 8 + i] for i in range(8)], axis=1)
        for k in range(2):
            rows = slice(k * BLOCK, (k + 1) * BLOCK)
            if k == 1:
                enter = (decays[0:1] * enter.astype(F32) + first[g]).astype(BF16)
            read = act_ref[rows, columns(INNER + GROUPS * STATE + g * STATE, STATE)]
            carried = jnp.dot(read, enter, preferred_element_type=F32) * widen(e2_ref[rows], g)
            mixed = (mix[rows, columns(g * 1024, 1024)] + carried).astype(BF16).astype(F32)
            mean = jnp.mean(mixed * mixed, axis=1, keepdims=True)
            normed = mixed * lax.rsqrt(mean + 1e-05) * gain_ref[:, columns(g * 1024, 1024)]
            out_ref[rows, columns(g * 1024, 1024)] = normed.astype(BF16)

    wait_all(state_out, 0)
    wait_all(decay_out, 2)
    wait_all(enter_out, 4)


def mixer(act, a, bt, lt, w2, e2, misc, gain):
    vmem = pl.BlockSpec(memory_space=pltpu.VMEM)
    return pl.pallas_call(
        mix_kernel,
        out_shape=jax.ShapeDtypeStruct((ROWS, INNER), BF16),
        in_specs=[vmem] * 8,
        out_specs=vmem,
        scratch_shapes=[
            pltpu.VMEM((GROUPS, 128, 1024), BF16),
            pltpu.VMEM((GROUPS, STATE, 1024), F32),
            pltpu.VMEM((ROWS, INNER), F32),
            pltpu.VMEM((3, 128, 128), F32),
            pltpu.VMEM((32, STATE, 128), BF16),
            pltpu.VMEM((32, 8, 128), F32),
            pltpu.VMEM((32, STATE, 128), BF16),
            pltpu.VMEM((32, 8, 128), F32),
            pltpu.VMEM((32, STATE, 128), BF16),
            pltpu.VMEM((32, STATE, 128), BF16),
            pltpu.SemaphoreType.DMA((6,)),
        ],
        compiler_params=pltpu.CompilerParams(
            collective_id=1, has_side_effects=True, vmem_limit_bytes=56 * 2**20
        ),
        name="mixer",
    )(act, a, bt, lt, w2, e2, misc, gain)


def per_device(
    tokens,
    in_weight,
    step_weight,
    step_bias,
    decay_rate,
    skip_gain,
    filter_taps,
    filter_bias,
    norm_gain,
):
    small = jnp.zeros((8, 128), F32)
    small = small.at[0:3, 0:HEADS].set(jnp.stack([step_bias, decay_rate, skip_gain]))
    act, a, bt, lt, w2, e2, misc = project(
        tokens, in_weight, step_weight, small, filter_taps, filter_bias[None]
    )
    bt = bt.reshape(8, 16, ROWS)
    lt = lt.reshape(8, 16, ROWS)
    return mixer(act, a, bt, lt, w2, e2, misc, norm_gain[None])[None]


def solution(mesh):
    in_specs = (P("dp", "ctx", None), P(None, "dp"), P(), P(), P(), P(), P(), P(), P())
    out_specs = P("dp", "ctx", None)
    return jax.shard_map(
        per_device, mesh=mesh, in_specs=in_specs, out_specs=out_specs, check_vma=False
    )
```

time: 633 us -> 103 us (0.16); the launches traced: 621 us -> 103 us
  waiting for transfers between devices: 222 us -> 0 us
  blocking collectives: 126 us -> 0 us
  matrix products: 98.5 us -> 0 us
  Pallas kernels: 0 us -> 94.5 us
  local copies, waits for them, and re-layouts: 93.8 us -> 6.65 us
  starting transfers between devices: 35.5 us -> 0 us
  other arithmetic: 31.2 us -> 1.29 us
  between operations: 13.9 us -> 0.02 us
    all_to_all x4 -> x0, waiting for transfers between devices: 137 us -> none  [the longest x1 58 us: per_device(): lax.all_to_all(partial_value, 'dp', split_axis=0, concat_axis=2, tiled=True)]
    all_to_all x2 -> x0, blocking collectives: 126 us -> none  [the longest x1 63.5 us: head_layout(): lax.all_to_all(value_parts, 'ctx', split_axis=1, concat_axis=0, tiled=True)]
    dot_general x28 -> x0, matrix products: 98.5 us -> none  [the longest x1 20.7 us: ssd_group(): jnp.einsum('khpn,ktn->kthp', entering, output_rows.astype(jnp.float32), p...]
    pallas_call x0 -> x2, Pallas kernels: none -> 94.5 us  [the longest x1 49.4 us: project(): pl.pallas_call(project_kernel, out_shape=(jax.ShapeDtypeStruct((ROWS, XBC...]
    all_gather x1 -> x0, waiting for transfers between devices: 83.8 us -> none  [per_device(): gathered = lax.all_gather(tokens, 'dp', axis=0, tiled=True)]
    convert_element_type x9 -> x0, local copies, waits for them, and re-layouts: 42.1 us -> none  [the longest x3 18.1 us: head_layout(): mixed_rows = pieces.reshape(full_length, local_width).astype(jnp.bfloat16)]
    all_to_all x4 -> x0, starting transfers between devices: 31.6 us -> none  [the longest x1 9.95 us: head_layout(): lax.all_to_all(step_parts, 'ctx', split_axis=1, concat_axis=0, tiled=True)]
    convert_element_type x6 -> x0, other arithmetic: 26.5 us -> none  [the longest x1 13.7 us: sequence_filter(): jax.nn.silu(filter_rows(rim_rows, projected, filter_taps, filter_bias))]
  transfers between devices with their start and end apart: 6 -> 0, of which waited for: 4 -> 0; matrix products, arithmetic and copies ran while one was open for 10% -> 0% of each run, Pallas kernels for 0% -> 0%
where the time goes in v1:
time: 103 us
  Pallas kernels  94.5 us (92%)
  local copies, waits for them, and re-layouts  6.65 us (6%)
  other arithmetic  1.29 us (1%)
    pallas_call x1, Pallas kernels, project(): pl.pallas_call(project_kernel, out_shape=(jax.ShapeDtypeStruct((ROWS, XBC...  49.4 us
    pallas_call x1, Pallas kernels, mixer(): pl.pallas_call(mix_kernel, out_shape=jax.ShapeDtypeStruct((ROWS, INNER),...  45.1 us
    unnamed x2, local copies, waits for them, and re-layouts  6.65 us

profile of v1, /device:TPU:24, one launch (start us, length us, event | category | flops | bytes accessed | tf_op | source)
XLA Modules:
  0.0 102.5 jit_solution(15073832546488232790)
XLA Ops:
  0.0 1.3 %select_maximum_fusion.small_ref = f32[8,128]{1,0:T(8,128)} fusion(f32[1,64]{1,0:T(1,128)} %bitcast.13, f32[1,64]{1,0:T(1,128)} %bitcast.14, f32[1,64]{1,0:T(1,128)} %bitcast.15), kind=kLoop, calls=%fused_computation | loop fusion | flops 11264 | bytes 4864 | tf_op jit(solution)/shard_map/stack | solution.py:600
  1.3 2.0 %copy.10.sw_ref = bf16[2048,64]{1,0:T(8,128)(2,1)} copy(bf16[2048,64]{0,1:T(8,128)(2,1)} %param.13) | data formatting | bytes 524288 | tf_op args[2]
  3.2 49.4 %project.1 = (bf16[512,5120]{1,0:T(8,128)(2,1)}, f32[4,512,128]{2,1,0:T(8,128)}, f32[128,512]{1,0:T(8,128)}, f32[128,512]{1,0:T(8,128)}, bf16[512,128]{1,0:T(8,1...) custom-call(bf16[1,512,2048]{2,1,0:T(8,128)(2,1)} %tok_ref.1, bf16[2048,1280]{1,0:T(8,128)(2,1)} %w_ref.1, ...), custom_call_target="tpu_custom_call" | custom-call | tf_op jit(solution)/shard_map/project/pallas_call | solution.py:380
  52.7 45.1 %mixer.1 = bf16[512,4096]{1,0:T(8,128)(2,1)} custom-call(bf16[512,5120]{1,0:T(8,128)(2,1)} %get-tuple-element.24.act_ref, f32[4,512,128]{2,1,0:T(8,128)} %get-tuple-element.25.a_ref, f32[8,16,512]{2,1,0:T(8,128)} %bitcast.9, f32[8,16,512]{2,1,0:T(8,128)} %bitcast.10, bf16[512,128]{1,0:T(8,128)(2,1)} %get-tuple-element.28.w2_ref, ...), custom_call_target="tpu_custom_call" | custom-call | tf_op jit(solution)/shard_map/mixer/pallas_call | solution.py:563
  97.8 4.7 %copy.12 = bf16[1,512,4096]{2,1,0:T(8,128)(2,1)} copy(bf16[1,512,4096]{2,1,0:T(8,128)(2,1)} %bitcast.8) | data formatting | bytes 8388608

commit v2 on v1

v2 whole, which is shorter than its diff:
```python
import functools

import jax
import jax.numpy as jnp
from jax import lax
from jax.experimental import pallas as pl
from jax.experimental.pallas import tpu as pltpu
from jax.sharding import PartitionSpec as P

D = 2048
HEADS = 64
HEAD_DIM = 64
STATE = 128
GROUPS = 4
BLOCK = 256
ROWS = 512
HALO = 16
SHARD = 1280
XBC = 5120
INNER = 4096
LOG2E = 1.4426950408889634
MESH = pl.DeviceIdType.MESH
F32 = jnp.float32
BF16 = jnp.bfloat16

RING_COL = ((0, 4, 1, 5), (2, 6, 3, 7))
SAME_SLOT = (10, 11, 14, 15, 16)
OTHER_SLOT = (12, 13, 17, 18, 19)
PEERS = 34


def same_slot(column):
    return 2 * SAME_SLOT[column // 2] + column % 2


def other_slot(column):
    return 2 * OTHER_SLOT[column // 2] + column % 2


def mixer_kernel(
    tok_ref, w_ref, sw_ref, bias_ref, rate_ref, skip_ref, taps_ref, fb_ref,
    out_ref,
    tok, wbuf, pbuf_a, pbuf_b, act, swp, small,
    a_ref, bt_ref, lt_ref, w2_ref, e2_ref, misc_ref,
    spread, first, mix, mixed_out, scores, totals, decays_in,
    state_out, state_in, enter_out, enter_in,
    loc_sem, tok_sem, out_sem, halo_sem, sib_send, sib_recv,
    x_send, x_recv, ring_send, ring_recv, fwd_send, fwd_recv, sems,
):
    dp = lax.axis_index("dp")
    ctx = lax.axis_index("ctx")
    z = ctx % 4
    y = (ctx // 4) % 4
    xh = ctx // 16
    sibling = dp + 1 - 2 * (dp % 2)
    across = (dp + 2) % 4
    place = (z, y)

    def along(dim, step):
        if dim == 0:
            return xh * 16 + y * 4 + (z + step) % 4
        return xh * 16 + ((y + step) % 4) * 4 + z

    source_a = (across, ctx)
    source_b = (across, (ctx + 16) % 32)
    after = (dp, (ctx + 1) % 32)

    def loc_copy(j):
        return pltpu.make_async_copy(
            w_ref.at[:, j * 128 : (j + 1) * 128], wbuf.at[j], loc_sem.at[j]
        )

    barrier = pltpu.get_barrier_semaphore()
    for peer in ((sibling, ctx), source_a, source_b):
        pl.semaphore_signal(barrier, inc=1, device_id=peer, device_id_type=MESH)

    @pl.loop(1, 32)
    def _(r):
        pl.semaphore_signal(
            barrier, inc=1, device_id=(dp, (ctx + r) % 32), device_id_type=MESH
        )

    tok_copy = pltpu.make_async_copy(tok_ref.at[0], tok.at[HALO:], tok_sem)
    tok_copy.start()
    for j in range(4):
        loc_copy(j).start()

    def remote(src, dst, send, recv, peer):
        return pltpu.make_async_remote_copy(
            src_ref=src, dst_ref=dst, send_sem=send, recv_sem=recv,
            device_id=peer, device_id_type=MESH,
        )

    def x_piece(dim, p):
        column = RING_COL[dim][p]
        rows = pl.ds(pl.multiple_of(place[dim] * 512, 512), 512)
        return remote(
            w_ref.at[rows, column * 128 : (column + 1) * 128],
            wbuf.at[same_slot(column), rows],
            x_send.at[dim * 4 + p], x_recv.at[dim * 4 + p],
            source_a if p < 2 else source_b,
        )

    def x_direct(k):
        column = 8 + k
        return remote(
            w_ref.at[:, column * 128 : (column + 1) * 128],
            wbuf.at[same_slot(column)],
            x_send.at[8 + k], x_recv.at[8 + k], (source_a, source_b)[k],
        )

    def ring_rows(dim, kind, p):
        back = (3, 1, 2)[kind]
        return pl.ds(pl.multiple_of(((place[dim] + back) % 4) * 512, 512), 512)

    def ring_out(dim, kind, p):
        column = RING_COL[dim][p]
        if kind == 0:
            rows, peer = pl.ds(pl.multiple_of(place[dim] * 512, 512), 512), along(dim, 1)
        elif kind == 1:
            rows, peer = pl.ds(pl.multiple_of(place[dim] * 512, 512), 512), along(dim, 3)
        elif p < 2:
            rows, peer = ring_rows(dim, 0, p), along(dim, 1)
        else:
            rows, peer = ring_rows(dim, 1, p), along(dim, 3)
        at = wbuf.at[same_slot(column), rows]
        index = dim * 12 + kind * 4 + p
        return remote(at, at, ring_send.at[index], ring_recv.at[index], (dp, peer))

    def ring_in(dim, kind, p):
        column = RING_COL[dim][p]
        at = wbuf.at[same_slot(column), ring_rows(dim, kind, p)]
        index = dim * 12 + kind * 4 + p
        return remote(at, at, ring_send.at[index], ring_recv.at[index], (dp, along(dim, 1)))

    def forward(index):
        if index in (8, 9):
            src, dst = wbuf.at[same_slot(index)], wbuf.at[other_slot(index)]
        else:
            if index < 8:
                dim, p = divmod(index, 4)
                rows = pl.ds(pl.multiple_of(place[dim] * 512, 512), 512)
            else:
                dim, rest = divmod(index - 10, 12)
                kind, p = divmod(rest, 4)
                rows = ring_rows(dim, kind, p)
            column = RING_COL[dim][p]
            src = wbuf.at[same_slot(column), rows]
            dst = wbuf.at[other_slot(column), rows]
        return remote(src, dst, fwd_send.at[index], fwd_recv.at[index], (sibling, ctx))

    def sib_copy(j):
        return remote(
            w_ref.at[:, j * 128 : (j + 1) * 128], wbuf.at[10 + j],
            sib_send.at[j], sib_recv.at[j], (sibling, ctx),
        )

    halo_copy = remote(
        tok_ref.at[0, ROWS - HALO :], tok.at[:HALO], halo_sem.at[0], halo_sem.at[1], after
    )

    pl.semaphore_wait(barrier, PEERS)
    for p, q in ((0, 2), (1, 3)):
        x_piece(0, p).start()
        x_piece(1, q).start()
        x_piece(1, p).start()
        x_piece(0, q).start()
    x_direct(0).start()
    x_direct(1).start()
    halo_copy.start()
    for j in range(4, 10):
        loc_copy(j).start()
    for j in range(10):
        sib_copy(j).start()

    swp[...] = jnp.zeros_like(swp)
    swp[0:HEADS] = sw_ref[...]
    small[...] = jnp.zeros_like(small)
    small[0:1, 0:HEADS] = bias_ref[...]
    small[1:2, 0:HEADS] = rate_ref[...]
    small[2:3, 0:HEADS] = skip_ref[...]
    tok_copy.wait()
    step_raw = lax.dot_general(
        tok[HALO:], swp[...], (((1,), (1,)), ((), ())), preferred_element_type=F32
    )
    step_raw = step_raw.astype(BF16).astype(F32) + small[0:1]
    step = jnp.maximum(step_raw, 0.0) + jnp.log1p(jnp.exp(-jnp.abs(step_raw)))
    keep = lax.broadcasted_iota(jnp.int32, (ROWS, 128), 1) < HEADS
    step = jnp.where(keep, step, 0.0)
    fall = step * (small[1:2] * (-LOG2E))
    lower = (
        lax.broadcasted_iota(jnp.int32, (BLOCK, BLOCK), 0)
        >= lax.broadcasted_iota(jnp.int32, (BLOCK, BLOCK), 1)
    ).astype(F32)
    level = jnp.log2(step)

    def halves(value):
        high = value.astype(BF16).astype(F32)
        low = (value - high).astype(BF16).astype(F32)
        return (high + pltpu.roll(low, 64, 1)).astype(BF16)

    ends = []
    for k in range(2):
        at = slice(k * BLOCK, (k + 1) * BLOCK)
        a = jnp.dot(
            lower, fall[at], precision=lax.Precision.HIGHEST, preferred_element_type=F32
        )
        end = a[BLOCK - 1 : BLOCK]
        ends.append(end)
        weight = jnp.where(keep[at], jnp.exp2(end - a) * step[at], 0.0)
        w2_ref[at] = halves(weight)
        e2_ref[at] = halves(jnp.where(keep[at], jnp.exp2(a), 0.0))
        turned = jnp.transpose(level[at] - a)
        turned_level = jnp.transpose(level[at])
        for g in range(GROUPS):
            a_ref[g, at] = a if g == 0 else pltpu.roll(a, 128 - 16 * g, 1)
            bt_ref[g, :, at] = turned[16 * g : 16 * g + 16]
            lt_ref[g, :, at] = turned_level[16 * g : 16 * g + 16]
    row = lax.broadcasted_iota(jnp.int32, (8, 128), 0)
    lane_ok = lax.broadcasted_iota(jnp.int32, (8, 128), 1) < HEADS
    exponent = jnp.where(row == 0, ends[0], jnp.where(row == 1, ends[1], ends[0] + ends[1]))
    rows_of = jnp.where(row == 3, small[2:3], jnp.exp2(exponent))
    misc_ref[...] = halves(jnp.where(lane_ok, rows_of, 0.0))

    head_row = lax.broadcasted_iota(jnp.int32, (128, 1024), 0) % HEADS
    head_lane = lax.broadcasted_iota(jnp.int32, (128, 1024), 1) // HEAD_DIM
    for g in range(GROUPS):
        spread[g] = (head_row == head_lane + 16 * g).astype(F32).astype(BF16)

    def total_send(r):
        peer = (ctx + r) % 32
        return remote(misc_ref, totals.at[ctx], sems.at[0], sems.at[1], (dp, peer))

    @pl.loop(1, 32)
    def _(r):
        total_send(r).start()

    totals[ctx] = misc_ref[...]

    halo_copy.wait_recv()

    @pl.when(ctx == 0)
    def _():
        tok[:HALO] = jnp.zeros((HALO, D), BF16)

    def x_arrive(dim, p):
        x_piece(dim, p).wait_recv()
        ring_out(dim, 0, p).start()
        ring_out(dim, 1, p).start()
        forward(dim * 4 + p).start()

    def near_arrive(dim, p):
        for kind in range(2):
            ring_in(dim, kind, p).wait_recv()
            if (kind == 0) == (p < 2):
                ring_out(dim, 2, p).start()
            forward(10 + dim * 12 + kind * 4 + p).start()

    def far_arrive(dim, p):
        ring_in(dim, 2, p).wait_recv()
        forward(10 + dim * 12 + 8 + p).start()

    def direct_arrive(k):
        x_direct(k).wait_recv()
        forward(8 + k).start()

    def other_wait(pieces):
        for dim, p in pieces:
            forward(dim * 4 + p).wait_recv()
            for kind in range(3):
                forward(10 + dim * 12 + kind * 4 + p).wait_recv()

    one = ((0, 0), (1, 2))
    two = ((1, 0), (0, 2))
    three = ((0, 1), (1, 3))
    four = ((1, 1), (0, 3))

    def events(ii):
        for n in range(5):
            @pl.when(ii == n)
            def _(n=n):
                for i in (2 * n, 2 * n + 1):
                    for j in (2 * i, 2 * i + 1):
                        if i < 5:
                            loc_copy(j).wait()
                        else:
                            sib_copy(j - 10).wait_recv()
                if n == 1:
                    for piece in one:
                        x_arrive(*piece)
                if n == 3:
                    for piece in two:
                        x_arrive(*piece)

        @pl.when(ii == 5)
        def _():
            for piece in three:
                x_arrive(*piece)
            for piece in one:
                near_arrive(*piece)
            for piece in four:
                x_arrive(*piece)
            for piece in two:
                near_arrive(*piece)
            for piece in one:
                far_arrive(*piece)
            for piece in two:
                far_arrive(*piece)

        @pl.when(ii == 6)
        def _():
            for piece in three:
                near_arrive(*piece)
            other_wait(((0, 0), (0, 2), (1, 0), (1, 2)))

        @pl.when(ii == 7)
        def _():
            for piece in four:
                near_arrive(*piece)
            for piece in three:
                far_arrive(*piece)
            for piece in four:
                far_arrive(*piece)

        @pl.when(ii == 8)
        def _():
            direct_arrive(0)
            direct_arrive(1)
            other_wait(((0, 1), (0, 3)))

        @pl.when(ii == 9)
        def _():
            other_wait(((1, 1), (1, 3)))
            forward(8).wait_recv()
            forward(9).wait_recv()

    def block_of(i):
        m = i - 10
        foreign = i // 10
        late = (i - 6) // 8 * foreign
        kind = foreign * (2 + (1 - late) * ((m % 4) // 2) + late * ((i - 14 + 30) // 3 - 10))
        near_kind = (1 - foreign) * (i // 5)
        pair = (1 - foreign) * (i % 5) + foreign * (
            (1 - late) * (m % 2) + late * (2 + (i - 14 + 30) % 3)
        )
        relation = kind + near_kind
        lo = (dp + relation) % 2
        hi = (dp // 2 + relation // 2) % 2
        return (2 * hi + lo) * 5 + pair

    def product(i, pbuf):
        weights = jnp.concatenate([wbuf[2 * i], wbuf[2 * i + 1]], axis=1)
        pbuf[...] = (
            jnp.dot(tok[...], weights, preferred_element_type=F32).astype(BF16).astype(F32)
        )

    def activate(block, at, pbuf):
        columns = pl.ds(pl.multiple_of(block * 256, 256), 256)
        taps = taps_ref[:, columns]
        summed = fb_ref[:, columns] + taps[0:1] * pbuf[HALO - 3 : HALO - 3 + ROWS]
        for k in range(1, 4):
            summed = summed + taps[k : k + 1] * pbuf[HALO - 3 + k : HALO - 3 + k + ROWS]
        half = 0.5 * summed
        act[at] = (half * jnp.tanh(half) + half).astype(BF16)

    pbuf_b[...] = jnp.zeros_like(pbuf_b)

    @pl.loop(0, 10)
    def _(ii):
        events(ii)
        i = 2 * ii
        started = (ii + 9) // 10
        block = block_of(i - started)
        at = started * block + (1 - started) * 20
        product(i, pbuf_a)
        activate(block, at, pbuf_b)
        product(i + 1, pbuf_b)
        activate(block_of(i), block_of(i), pbuf_a)

    activate(block_of(19), block_of(19), pbuf_b)

    def widen(value, g):
        return jnp.dot(value, spread[g], preferred_element_type=F32)

    def group_of(g, at):
        return jnp.concatenate([act[4 * g + j, at] for j in range(4)], axis=1)

    def map_lanes(g, at, base):
        return act[base + g // 2, at, pl.ds(pl.multiple_of((g % 2) * 128, 128), 128)]

    def state_send(r, half):
        peer = (ctx + r) % 32
        rows = slice(half * 64, half * 64 + 64)
        return remote(
            state_out.at[peer, rows], state_in.at[half, ctx],
            sems.at[2 + half], sems.at[4 + half], (dp, peer),
        )

    def enter_send(r, half):
        peer = (ctx + r) % 32
        rows = slice(half * 64, half * 64 + 64)
        return remote(
            enter_out.at[half, peer], enter_in.at[ctx, rows],
            sems.at[6 + half], sems.at[8 + half], (dp, peer),
        )

    def wait_all(part, index):
        pltpu.make_async_copy(part, part, sems.at[index]).wait()

    @pl.loop(0, GROUPS)
    def _(g):
        decays = widen(misc_ref[...], g)
        total = None
        for k in range(2):
            at = slice(k * BLOCK, (k + 1) * BLOCK)
            values = group_of(g, at).astype(F32)
            scaled = (widen(w2_ref[at], g) * values).astype(BF16)
            maps = map_lanes(g, at, 16)
            state = lax.dot_general(
                maps, scaled, (((0,), (0,)), ((), ())), preferred_element_type=F32
            )
            if k == 0:
                first[g] = state
                total = decays[1:2] * state
            else:
                total = total + state
        for i in range(8):
            state_out[g * 8 + i] = total[:, i * 128 : (i + 1) * 128].astype(BF16)

    for half in range(2):
        @pl.loop(1, 32)
        def _(r):
            state_send(r, half).start()

        state_in[half, ctx] = state_out[ctx, half * 64 : half * 64 + 64]

    lane = lax.broadcasted_iota(jnp.int32, (BLOCK, 128), 1) < HEAD_DIM
    causal = lax.broadcasted_iota(jnp.int32, (128, 128), 0) >= lax.broadcasted_iota(
        jnp.int32, (128, 128), 1
    )

    @pl.loop(0, 8)
    def _(n):
        g = n // 2
        start = (n % 2) * BLOCK
        rows = pl.ds(pl.multiple_of(start, BLOCK), BLOCK)
        early = pl.ds(pl.multiple_of(start, 128), 128)
        later = pl.ds(pl.multiple_of(start + 128, 128), 128)
        full = lax.dot_general(
            map_lanes(g, rows, 18), map_lanes(g, rows, 16),
            (((1,), (1,)), ((), ())), preferred_element_type=F32,
        )
        scores[0] = jnp.where(causal, full[:128, :128], 0.0)
        scores[1] = full[128:, :128]
        scores[2] = jnp.where(causal, full[128:, 128:], 0.0)
        skip = widen(misc_ref[...], g)[3:4]
        for i in range(8):
            lanes = slice((i % 2) * 128, (i % 2) * 128 + 128)
            values = act[4 * g + i // 2, rows, lanes]
            made = []
            for h in (2 * i, 2 * i + 1):
                upper = a_ref[g, early, h : h + 1]
                under = a_ref[g, later, h : h + 1]
                b0 = bt_ref[g, h : h + 1, early]
                b1 = bt_ref[g, h : h + 1, later]
                l0 = lt_ref[g, h : h + 1, early]
                l1 = lt_ref[g, h : h + 1, later]
                w00 = (jnp.exp2(jnp.minimum(upper + b0, l0)) * scores[0]).astype(BF16)
                w10 = (jnp.exp2(under + b0) * scores[1]).astype(BF16)
                w11 = (jnp.exp2(jnp.minimum(under + b1, l1)) * scores[2]).astype(BF16)
                top = jnp.dot(w00, values[:128], preferred_element_type=F32)
                low = jnp.dot(
                    jnp.concatenate([w10, w11], axis=1), values, preferred_element_type=F32
                )
                made.append(jnp.concatenate([top, low], axis=0))
            mixed = jnp.where(lane, made[0], made[1])
            mix[g, rows, i * 128 : (i + 1) * 128] = (
                mixed + skip[:, i * 128 : (i + 1) * 128] * values.astype(F32)
            )

    wait_all(totals.at[0:31], 1)
    mine = lax.broadcasted_iota(jnp.int32, (128, 128), 0) % HEADS == (
        2 * ctx + lax.broadcasted_iota(jnp.int32, (128, 128), 1) // HEAD_DIM
    )
    pick = mine.astype(F32).astype(BF16)
    for k in range(32):
        decays_in[k] = jnp.dot(totals[k], pick, preferred_element_type=F32)

    for half in range(2):
        wait_all(state_in.at[half, 0:31], 4 + half)

        def scan(k, carry):
            enter_out[half, k] = carry.astype(BF16)
            return decays_in[k, 2:3] * carry + state_in[half, k].astype(F32)

        lax.fori_loop(0, 32, scan, jnp.zeros((64, 128), F32))

        @pl.loop(1, 32)
        def _(r):
            enter_send(r, half).start()

        enter_in[ctx, half * 64 : half * 64 + 64] = enter_out[half, ctx]

    for half in range(2):
        wait_all(enter_in.at[0:31, half * 64 : half * 64 + 64], 8 + half)

    def out_copy(g):
        columns = pl.ds(pl.multiple_of(g * 1024, 1024), 1024)
        return pltpu.make_async_copy(mixed_out.at[g], out_ref.at[:, columns], out_sem)

    @pl.loop(0, GROUPS)
    def _(g):
        decays = widen(misc_ref[...], g)
        enter = jnp.concatenate([enter_in[g * 8 + i] for i in range(8)], axis=1)
        for k in range(2):
            rows = slice(k * BLOCK, (k + 1) * BLOCK)
            if k == 1:
                enter = (decays[0:1] * enter.astype(F32) + first[g]).astype(BF16)
            carried = jnp.dot(
                map_lanes(g, rows, 18), enter, preferred_element_type=F32
            ) * widen(e2_ref[rows], g)
            mixed_out[g, rows] = (mix[g, rows] + carried).astype(BF16)
        out_copy(g).start()

    halo_copy.wait_send()
    for dim in range(2):
        for p in range(4):
            x_piece(dim, p).wait_send()
            for kind in range(3):
                ring_out(dim, kind, p).wait_send()
    for k in range(2):
        x_direct(k).wait_send()
    for j in range(10):
        sib_copy(j).wait_send()
    for index in range(34):
        forward(index).wait_send()
    wait_all(totals.at[0:31], 0)
    for half in range(2):
        wait_all(state_in.at[half, 0:31], 2 + half)
        wait_all(state_in.at[half, 0:31], 6 + half)
    pltpu.make_async_copy(mixed_out, mixed_out, out_sem).wait()


def mixer(tokens, in_weight, step_weight, bias, rate, skip, taps, filter_bias):
    vmem = pl.BlockSpec(memory_space=pltpu.VMEM)
    anywhere = pl.BlockSpec(memory_space=pl.ANY)
    dma = pltpu.SemaphoreType.DMA
    return pl.pallas_call(
        mixer_kernel,
        out_shape=jax.ShapeDtypeStruct((ROWS, INNER), BF16),
        in_specs=[anywhere, anywhere] + [vmem] * 6,
        out_specs=anywhere,
        scratch_shapes=[
            pltpu.VMEM((HALO + ROWS, D), BF16),
            pltpu.VMEM((40, D, 128), BF16),
            pltpu.VMEM((HALO + ROWS, 256), F32),
            pltpu.VMEM((HALO + ROWS, 256), F32),
            pltpu.VMEM((21, ROWS, 256), BF16),
            pltpu.VMEM((128, D), BF16),
            pltpu.VMEM((8, 128), F32),
            pltpu.VMEM((GROUPS, ROWS, 128), F32),
            pltpu.VMEM((GROUPS, 16, ROWS), F32),
            pltpu.VMEM((GROUPS, 16, ROWS), F32),
            pltpu.VMEM((ROWS, 128), BF16),
            pltpu.VMEM((ROWS, 128), BF16),
            pltpu.VMEM((8, 128), BF16),
            pltpu.VMEM((GROUPS, 128, 1024), BF16),
            pltpu.VMEM((GROUPS, STATE, 1024), F32),
            pltpu.VMEM((GROUPS, ROWS, 1024), F32),
            pltpu.VMEM((GROUPS, ROWS, 1024), BF16),
            pltpu.VMEM((3, 128, 128), F32),
            pltpu.VMEM((32, 8, 128), BF16),
            pltpu.VMEM((32, 8, 128), F32),
            pltpu.VMEM((32, STATE, 128), BF16),
            pltpu.VMEM((2, 32, 64, 128), BF16),
            pltpu.VMEM((2, 32, 64, 128), BF16),
            pltpu.VMEM((32, STATE, 128), BF16),
            dma((10,)), dma, dma, dma((2,)), dma((10,)), dma((10,)),
            dma((10,)), dma((10,)), dma((24,)), dma((24,)), dma((34,)), dma((34,)), dma((10,)),
        ],
        compiler_params=pltpu.CompilerParams(
            collective_id=0, has_side_effects=True, vmem_limit_bytes=58 * 2**20
        ),
        name="mixer",
    )(tokens, in_weight, step_weight, bias, rate, skip, taps, filter_bias)


def norm_kernel(mixed_ref, gain_ref, out_ref):
    for g in range(GROUPS):
        columns = slice(g * 1024, (g + 1) * 1024)
        mixed = mixed_ref[:, columns].astype(F32)
        mean = jnp.mean(mixed * mixed, axis=1, keepdims=True)
        out_ref[:, columns] = (mixed * lax.rsqrt(mean + 1e-05) * gain_ref[:, columns]).astype(
            BF16
        )


def group_norm(mixed, gain):
    tile = 64
    return pl.pallas_call(
        norm_kernel,
        out_shape=jax.ShapeDtypeStruct((ROWS, INNER), BF16),
        grid=(ROWS // tile,),
        in_specs=[
            pl.BlockSpec((tile, INNER), lambda i: (i, 0)),
            pl.BlockSpec((1, INNER), lambda i: (0, 0)),
        ],
        out_specs=pl.BlockSpec((tile, INNER), lambda i: (i, 0)),
        name="group_norm",
    )(mixed, gain)


def per_device(
    tokens,
    in_weight,
    step_weight,
    step_bias,
    decay_rate,
    skip_gain,
    filter_taps,
    filter_bias,
    norm_gain,
):
    mixed = mixer(
        tokens, in_weight, step_weight.T, step_bias[None], decay_rate[None], skip_gain[None],
        filter_taps, filter_bias[None],
    )
    return group_norm(mixed, norm_gain[None])[None]


def solution(mesh):
    in_specs = (P("dp", "ctx", None), P(None, "dp"), P(), P(), P(), P(), P(), P(), P())
    out_specs = P("dp", "ctx", None)
    return jax.shard_map(
        per_device, mesh=mesh, in_specs=in_specs, out_specs=out_specs, check_vma=False
    )
```

time: 103 us -> 117 us (1.14)
  Pallas kernels: 94.5 us -> 117 us
  local copies, waits for them, and re-layouts: 6.65 us -> 0 us
  other arithmetic: 1.29 us -> 0 us
    pallas_call x2, Pallas kernels: 94.5 us -> 117 us  [the longest x1 109 us: mixer(): pl.pallas_call(mixer_kernel, out_shape=jax.ShapeDtypeStruct((ROWS, INNER)...]
    unnamed x2 -> x0, local copies, waits for them, and re-layouts: 6.65 us -> none
    another operation x1 -> x0, other arithmetic: 1.29 us -> none  [per_device(): jnp.stack([step_bias, decay_rate, skip_gain])]
where the time goes in v2:
time: 117 us
  Pallas kernels  117 us (100%)
    pallas_call x1, Pallas kernels, mixer(): pl.pallas_call(mixer_kernel, out_shape=jax.ShapeDtypeStruct((ROWS, INNER)...  109 us
    pallas_call x1, Pallas kernels, group_norm(): pl.pallas_call(norm_kernel, out_shape=jax.ShapeDtypeStruct((ROWS, INNER),...  7.28 us

profile of v2, /device:TPU:24, one launch (start us, length us, event | category | flops | bytes accessed | tf_op | source)
XLA Modules:
  0.0 116.6 jit_solution(10851489782610370178)
XLA Ops:
  0.0 109.3 %mixer.1.mixed_ref = bf16[512,4096]{1,0:T(8,128)(2,1)} custom-call(bf16[1,512,2048]{2,1,0:T(8,128)(2,1)} %tok_ref.1, bf16[2048,1280]{1,0:T(8,128)(2,1)} %w_ref.1, bf16[64,2048]{1,0:T(8,128)(2,1)} %bitcast.7, f32[1,64]{1,0:T(1,128)} %bitcast.10, f32[1,64]{1,0:T(1,128)} %bitcast.11, f32[1,64]{1,0:T(1,128)} %bitcast.12, f32[4,5120]{1,0:T(4,128)} %taps_ref.1, ...), custom_call_target="tpu_custom_call" | custom-call | tf_op jit(solution)/shard_map/mixer/pallas_call | solution.py:548
  109.3 7.3 %group_norm.1 = bf16[512,4096]{1,0:T(8,128)(2,1)} custom-call(bf16[512,4096]{1,0:T(8,128)(2,1)} %mixer.1.mixed_ref, f32[1,4096]{1,0:T(1,128)} %bitcast.9), custom_call_target="tpu_custom_call" | custom-call | tf_op jit(solution)/shard_map/group_norm/pallas_call | solution.py:600

commit v3 on v2

--- a/solution.py
+++ b/solution.py
@@ -40,7 +40,7 @@
 def mixer_kernel(
     tok_ref, w_ref, sw_ref, bias_ref, rate_ref, skip_ref, taps_ref, fb_ref,
     out_ref,
-    tok, wbuf, pbuf_a, pbuf_b, act, swp, small,
+    tok, wbuf, pbuf, act, swp, small,
     a_ref, bt_ref, lt_ref, w2_ref, e2_ref, misc_ref,
     spread, first, mix, mixed_out, scores, totals, decays_in,
     state_out, state_in, enter_out, enter_in,
@@ -115,14 +115,8 @@
 
     def ring_out(dim, kind, p):
         column = RING_COL[dim][p]
-        if kind == 0:
-            rows, peer = pl.ds(pl.multiple_of(place[dim] * 512, 512), 512), along(dim, 1)
-        elif kind == 1:
-            rows, peer = pl.ds(pl.multiple_of(place[dim] * 512, 512), 512), along(dim, 3)
-        elif p < 2:
-            rows, peer = ring_rows(dim, 0, p), along(dim, 1)
-        else:
-            rows, peer = ring_rows(dim, 1, p), along(dim, 3)
+        rows = pl.ds(pl.multiple_of(place[dim] * 512, 512), 512)
+        peer = along(dim, (1, 3, 2)[kind])
         at = wbuf.at[same_slot(column), rows]
         index = dim * 12 + kind * 4 + p
         return remote(at, at, ring_send.at[index], ring_recv.at[index], (dp, peer))
@@ -159,7 +153,9 @@
         tok_ref.at[0, ROWS - HALO :], tok.at[:HALO], halo_sem.at[0], halo_sem.at[1], after
     )
 
-    pl.semaphore_wait(barrier, PEERS)
+    with jax.named_scope("barrier"):
+        pl.semaphore_wait(barrier, PEERS)
+    halo_copy.start()
     for p, q in ((0, 2), (1, 3)):
         x_piece(0, p).start()
         x_piece(1, q).start()
@@ -167,7 +163,6 @@
         x_piece(0, q).start()
     x_direct(0).start()
     x_direct(1).start()
-    halo_copy.start()
     for j in range(4, 10):
         loc_copy(j).start()
     for j in range(10):
@@ -179,7 +174,8 @@
     small[0:1, 0:HEADS] = bias_ref[...]
     small[1:2, 0:HEADS] = rate_ref[...]
     small[2:3, 0:HEADS] = skip_ref[...]
-    tok_copy.wait()
+    with jax.named_scope("tokwait"):
+        tok_copy.wait()
     step_raw = lax.dot_general(
         tok[HALO:], swp[...], (((1,), (1,)), ((), ())), preferred_element_type=F32
     )
@@ -237,7 +233,8 @@
 
     totals[ctx] = misc_ref[...]
 
-    halo_copy.wait_recv()
+    with jax.named_scope("halowait"):
+        halo_copy.wait_recv()
 
     @pl.when(ctx == 0)
     def _():
@@ -247,13 +244,12 @@
         x_piece(dim, p).wait_recv()
         ring_out(dim, 0, p).start()
         ring_out(dim, 1, p).start()
+        ring_out(dim, 2, p).start()
         forward(dim * 4 + p).start()
 
     def near_arrive(dim, p):
         for kind in range(2):
             ring_in(dim, kind, p).wait_recv()
-            if (kind == 0) == (p < 2):
-                ring_out(dim, 2, p).start()
             forward(10 + dim * 12 + kind * 4 + p).start()
 
     def far_arrive(dim, p):
@@ -275,62 +271,57 @@
     three = ((0, 1), (1, 3))
     four = ((1, 1), (0, 3))
 
-    def events(ii):
+    def events(i):
         for n in range(5):
-            @pl.when(ii == n)
+            @pl.when(i == n)
             def _(n=n):
-                for i in (2 * n, 2 * n + 1):
-                    for j in (2 * i, 2 * i + 1):
-                        if i < 5:
-                            loc_copy(j).wait()
-                        else:
-                            sib_copy(j - 10).wait_recv()
-                if n == 1:
-                    for piece in one:
-                        x_arrive(*piece)
-                if n == 3:
-                    for piece in two:
-                        x_arrive(*piece)
-
-        @pl.when(ii == 5)
+                loc_copy(2 * n).wait()
+                loc_copy(2 * n + 1).wait()
+
+            @pl.when(i == 5 + n)
+            def _(n=n):
+                sib_copy(2 * n).wait_recv()
+                sib_copy(2 * n + 1).wait_recv()
+
+        def at(step, *actions):
+            @pl.when(i == step)
+            def _():
+                for action, pieces in actions:
+                    for piece in pieces:
+                        action(*piece)
+
+        at(1, (x_arrive, one))
+        at(4, (x_arrive, two))
+        at(7, (x_arrive, three))
+        at(9, (x_arrive, four), (near_arrive, one))
+        at(10, (near_arrive, two), (far_arrive, one), (far_arrive, two))
+        at(11, (near_arrive, three))
+
+        @pl.when(i == 12)
         def _():
-            for piece in three:
-                x_arrive(*piece)
-            for piece in one:
-                near_arrive(*piece)
-            for piece in four:
-                x_arrive(*piece)
-            for piece in two:
-                near_arrive(*piece)
-            for piece in one:
-                far_arrive(*piece)
-            for piece in two:
-                far_arrive(*piece)
-
-        @pl.when(ii == 6)
+            other_wait(((0, 0), (0, 2)))
+
+        @pl.when(i == 13)
         def _():
-            for piece in three:
-                near_arrive(*piece)
-            other_wait(((0, 0), (0, 2), (1, 0), (1, 2)))
-
-        @pl.when(ii == 7)
-        def _():
-            for piece in four:
-                near_arrive(*piece)
-            for piece in three:
-                far_arrive(*piece)
-            for piece in four:
-                far_arrive(*piece)
-
-        @pl.when(ii == 8)
+            other_wait(((1, 0), (1, 2)))
+
+        at(14, (near_arrive, four), (far_arrive, three), (far_arrive, four))
+
+        @pl.when(i == 15)
         def _():
             direct_arrive(0)
             direct_arrive(1)
+
+        @pl.when(i == 17)
+        def _():
             other_wait(((0, 1), (0, 3)))
 
-        @pl.when(ii == 9)
+        @pl.when(i == 18)
         def _():
             other_wait(((1, 1), (1, 3)))
+
+        @pl.when(i == 19)
+        def _():
             forward(8).wait_recv()
             forward(9).wait_recv()
 
@@ -348,36 +339,31 @@
         hi = (dp // 2 + relation // 2) % 2
         return (2 * hi + lo) * 5 + pair
 
-    def product(i, pbuf):
-        weights = jnp.concatenate([wbuf[2 * i], wbuf[2 * i + 1]], axis=1)
-        pbuf[...] = (
-            jnp.dot(tok[...], weights, preferred_element_type=F32).astype(BF16).astype(F32)
-        )
-
-    def activate(block, at, pbuf):
-        columns = pl.ds(pl.multiple_of(block * 256, 256), 256)
-        taps = taps_ref[:, columns]
-        summed = fb_ref[:, columns] + taps[0:1] * pbuf[HALO - 3 : HALO - 3 + ROWS]
-        for k in range(1, 4):
-            summed = summed + taps[k : k + 1] * pbuf[HALO - 3 + k : HALO - 3 + k + ROWS]
-        half = 0.5 * summed
-        act[at] = (half * jnp.tanh(half) + half).astype(BF16)
-
-    pbuf_b[...] = jnp.zeros_like(pbuf_b)
-
-    @pl.loop(0, 10)
-    def _(ii):
-        events(ii)
-        i = 2 * ii
-        started = (ii + 9) // 10
-        block = block_of(i - started)
-        at = started * block + (1 - started) * 20
-        product(i, pbuf_a)
-        activate(block, at, pbuf_b)
-        product(i + 1, pbuf_b)
-        activate(block_of(i), block_of(i), pbuf_a)
-
-    activate(block_of(19), block_of(19), pbuf_b)
+    @pl.loop(0, 20)
+    def _(i):
+        with jax.named_scope("events"):
+            events(i)
+        with jax.named_scope("compute"):
+            block = block_of(i)
+            weights = jnp.concatenate([wbuf[2 * i], wbuf[2 * i + 1]], axis=1)
+            result = jnp.dot(tok[...], weights, preferred_element_type=F32)
+            result = result.astype(BF16).astype(F32)
+            for side in range(2):
+                pbuf[side] = result[:, side * 128 : side * 128 + 128]
+            for side in range(2):
+                lanes = pl.ds(pl.multiple_of(block * 256 + side * 128, 128), 128)
+                taps = taps_ref[:, lanes]
+                bias = fb_ref[:, lanes]
+                for row in range(0, ROWS, 64):
+                    at = HALO - 3 + row
+                    summed = bias + taps[0:1] * pbuf[side, at : at + 64]
+                    for k in range(1, 4):
+                        summed = summed + taps[k : k + 1] * pbuf[side, at + k : at + k + 64]
+                    half = 0.5 * summed
+                    act[block, row : row + 64, side * 128 : side * 128 + 128] = (
+                        half * jnp.tanh(half) + half
+                    ).astype(BF16)
+
 
     def widen(value, g):
         return jnp.dot(value, spread[g], preferred_element_type=F32)
@@ -408,6 +394,7 @@
         pltpu.make_async_copy(part, part, sems.at[index]).wait()
 
     @pl.loop(0, GROUPS)
+    @jax.named_scope("groups")
     def _(g):
         decays = widen(misc_ref[...], g)
         total = None
@@ -440,6 +427,7 @@
     )
 
     @pl.loop(0, 8)
+    @jax.named_scope("within")
     def _(n):
         g = n // 2
         start = (n % 2) * BLOCK
@@ -478,7 +466,8 @@
                 mixed + skip[:, i * 128 : (i + 1) * 128] * values.astype(F32)
             )
 
-    wait_all(totals.at[0:31], 1)
+    with jax.named_scope("totals"):
+        wait_all(totals.at[0:31], 1)
     mine = lax.broadcasted_iota(jnp.int32, (128, 128), 0) % HEADS == (
         2 * ctx + lax.broadcasted_iota(jnp.int32, (128, 128), 1) // HEAD_DIM
     )
@@ -487,7 +476,8 @@
         decays_in[k] = jnp.dot(totals[k], pick, preferred_element_type=F32)
 
     for half in range(2):
-        wait_all(state_in.at[half, 0:31], 4 + half)
+        with jax.named_scope("statewait"):
+            wait_all(state_in.at[half, 0:31], 4 + half)
 
         def scan(k, carry):
             enter_out[half, k] = carry.astype(BF16)
@@ -502,13 +492,15 @@
         enter_in[ctx, half * 64 : half * 64 + 64] = enter_out[half, ctx]
 
     for half in range(2):
-        wait_all(enter_in.at[0:31, half * 64 : half * 64 + 64], 8 + half)
+        with jax.named_scope("enterwait"):
+            wait_all(enter_in.at[0:31, half * 64 : half * 64 + 64], 8 + half)
 
     def out_copy(g):
         columns = pl.ds(pl.multiple_of(g * 1024, 1024), 1024)
         return pltpu.make_async_copy(mixed_out.at[g], out_ref.at[:, columns], out_sem)
 
     @pl.loop(0, GROUPS)
+    @jax.named_scope("groups")
     def _(g):
         decays = widen(misc_ref[...], g)
         enter = jnp.concatenate([enter_in[g * 8 + i] for i in range(8)], axis=1)
@@ -522,23 +514,24 @@
             mixed_out[g, rows] = (mix[g, rows] + carried).astype(BF16)
         out_copy(g).start()
 
-    halo_copy.wait_send()
-    for dim in range(2):
-        for p in range(4):
-            x_piece(dim, p).wait_send()
-            for kind in range(3):
-                ring_out(dim, kind, p).wait_send()
-    for k in range(2):
-        x_direct(k).wait_send()
-    for j in range(10):
-        sib_copy(j).wait_send()
-    for index in range(34):
-        forward(index).wait_send()
-    wait_all(totals.at[0:31], 0)
-    for half in range(2):
-        wait_all(state_in.at[half, 0:31], 2 + half)
-        wait_all(state_in.at[half, 0:31], 6 + half)
-    pltpu.make_async_copy(mixed_out, mixed_out, out_sem).wait()
+    with jax.named_scope("drain"):
+        halo_copy.wait_send()
+        for dim in range(2):
+            for p in range(4):
+                x_piece(dim, p).wait_send()
+                for kind in range(3):
+                    ring_out(dim, kind, p).wait_send()
+        for k in range(2):
+            x_direct(k).wait_send()
+        for j in range(10):
+            sib_copy(j).wait_send()
+        for index in range(34):
+            forward(index).wait_send()
+        wait_all(totals.at[0:31], 0)
+        for half in range(2):
+            wait_all(state_in.at[half, 0:31], 2 + half)
+            wait_all(state_in.at[half, 0:31], 6 + half)
+        pltpu.make_async_copy(mixed_out, mixed_out, out_sem).wait()
 
 
 def mixer(tokens, in_weight, step_weight, bias, rate, skip, taps, filter_bias):
@@ -553,9 +546,8 @@
         scratch_shapes=[
             pltpu.VMEM((HALO + ROWS, D), BF16),
             pltpu.VMEM((40, D, 128), BF16),
-            pltpu.VMEM((HALO + ROWS, 256), F32),
-            pltpu.VMEM((HALO + ROWS, 256), F32),
-            pltpu.VMEM((21, ROWS, 256), BF16),
+            pltpu.VMEM((2, HALO + ROWS, 128), F32),
+            pltpu.VMEM((20, ROWS, 256), BF16),
             pltpu.VMEM((128, D), BF16),
             pltpu.VMEM((8, 128), F32),
             pltpu.VMEM((GROUPS, ROWS, 128), F32),
@@ -596,7 +588,7 @@
 
 
 def group_norm(mixed, gain):
-    tile = 64
+    tile = 256
     return pl.pallas_call(
         norm_kernel,
         out_shape=jax.ShapeDtypeStruct((ROWS, INNER), BF16),

time: 117 us -> 86.8 us (0.74)
  Pallas kernels: 117 us -> 86.7 us
    pallas_call x1, Pallas kernels: 109 us -> 82.2 us  [mixer(): pl.pallas_call(mixer_kernel, out_shape=jax.ShapeDtypeStruct((ROWS, INNER)...]
    pallas_call x1, Pallas kernels: 7.28 us -> 4.53 us  [group_norm(): pl.pallas_call(norm_kernel, out_shape=jax.ShapeDtypeStruct((ROWS, INNER),...]
where the time goes in v3:
time: 86.8 us; the launch traced here: 86.7 us
  Pallas kernels  86.7 us (100%)
    pallas_call x1, Pallas kernels, mixer(): pl.pallas_call(mixer_kernel, out_shape=jax.ShapeDtypeStruct((ROWS, INNER)...  82.2 us
    pallas_call x1, Pallas kernels, group_norm(): pl.pallas_call(norm_kernel, out_shape=jax.ShapeDtypeStruct((ROWS, INNER),...  4.53 us

profile of v3, /device:TPU:24, one launch (start us, length us, event | category | flops | bytes accessed | tf_op | source)
XLA Modules:
  0.0 86.7 jit_solution(18050040667870206805)
XLA Ops:
  0.0 82.2 %mixer.1.mixed_ref = bf16[512,4096]{1,0:T(8,128)(2,1)} custom-call(bf16[1,512,2048]{2,1,0:T(8,128)(2,1)} %tok_ref.1, bf16[2048,1280]{1,0:T(8,128)(2,1)} %w_ref.1, bf16[64,2048]{1,0:T(8,128)(2,1)} %bitcast.7, f32[1,64]{1,0:T(1,128)} %bitcast.10, f32[1,64]{1,0:T(1,128)} %bitcast.11, f32[1,64]{1,0:T(1,128)} %bitcast.12, f32[4,5120]{1,0:T(4,128)} %taps_ref.1, ...), custom_call_target="tpu_custom_call" | custom-call | tf_op jit(solution)/shard_map/mixer/pallas_call | solution.py:541
  82.2 4.5 %group_norm.1 = bf16[512,4096]{1,0:T(8,128)(2,1)} custom-call(bf16[512,4096]{1,0:T(8,128)(2,1)} %mixer.1.mixed_ref, f32[1,4096]{1,0:T(1,128)} %bitcast.9), custom_call_target="tpu_custom_call" | custom-call | tf_op jit(solution)/shard_map/group_norm/pallas_call | solution.py:592

commit v4 on v3

--- a/solution.py
+++ b/solution.py
@@ -23,9 +23,9 @@
 F32 = jnp.float32
 BF16 = jnp.bfloat16
 
-RING_COL = ((0, 4, 1, 5), (2, 6, 3, 7))
-SAME_SLOT = (10, 11, 14, 15, 16)
-OTHER_SLOT = (12, 13, 17, 18, 19)
+RING_COL = ((0, 4, 3, 7), (2, 6, 1, 5))
+SAME_SLOT = (10, 12, 14, 16, 18)
+OTHER_SLOT = (11, 13, 15, 17, 19)
 PEERS = 34
 
 
@@ -116,7 +116,9 @@
     def ring_out(dim, kind, p):
         column = RING_COL[dim][p]
         rows = pl.ds(pl.multiple_of(place[dim] * 512, 512), 512)
-        peer = along(dim, (1, 3, 2)[kind])
+        peer = along(dim, (1, 3, 1 if p < 2 else 3)[kind])
+        if kind == 2:
+            rows = ring_rows(dim, 0 if p < 2 else 1, p)
         at = wbuf.at[same_slot(column), rows]
         index = dim * 12 + kind * 4 + p
         return remote(at, at, ring_send.at[index], ring_recv.at[index], (dp, peer))
@@ -244,12 +246,13 @@
         x_piece(dim, p).wait_recv()
         ring_out(dim, 0, p).start()
         ring_out(dim, 1, p).start()
-        ring_out(dim, 2, p).start()
         forward(dim * 4 + p).start()
 
     def near_arrive(dim, p):
         for kind in range(2):
             ring_in(dim, kind, p).wait_recv()
+            if (kind == 0) == (p < 2):
+                ring_out(dim, 2, p).start()
             forward(10 + dim * 12 + kind * 4 + p).start()
 
     def far_arrive(dim, p):
@@ -290,35 +293,22 @@
                     for piece in pieces:
                         action(*piece)
 
-        at(1, (x_arrive, one))
-        at(4, (x_arrive, two))
-        at(7, (x_arrive, three))
-        at(9, (x_arrive, four), (near_arrive, one))
-        at(10, (near_arrive, two), (far_arrive, one), (far_arrive, two))
-        at(11, (near_arrive, three))
-
-        @pl.when(i == 12)
-        def _():
-            other_wait(((0, 0), (0, 2)))
-
-        @pl.when(i == 13)
-        def _():
-            other_wait(((1, 0), (1, 2)))
-
-        at(14, (near_arrive, four), (far_arrive, three), (far_arrive, four))
-
-        @pl.when(i == 15)
-        def _():
-            direct_arrive(0)
-            direct_arrive(1)
-
-        @pl.when(i == 17)
-        def _():
-            other_wait(((0, 1), (0, 3)))
-
-        @pl.when(i == 18)
-        def _():
-            other_wait(((1, 1), (1, 3)))
+        def other(pieces):
+            other_wait(pieces)
+
+        at(2, (x_arrive, one))
+        at(5, (x_arrive, two))
+        at(7, (near_arrive, one))
+        at(8, (x_arrive, three))
+        at(9, (near_arrive, two))
+        at(10, (x_arrive, four), (far_arrive, one))
+        at(11, (near_arrive, three), (other, ((one,),)))
+        at(12, (far_arrive, two))
+        at(13, (near_arrive, four), (other, ((two,),)))
+        at(14, (far_arrive, three))
+        at(15, (other, ((three,),)))
+        at(16, (far_arrive, four), (direct_arrive, ((0,), (1,))))
+        at(17, (other, ((four,),)))
 
         @pl.when(i == 19)
         def _():
@@ -326,15 +316,9 @@
             forward(9).wait_recv()
 
     def block_of(i):
-        m = i - 10
         foreign = i // 10
-        late = (i - 6) // 8 * foreign
-        kind = foreign * (2 + (1 - late) * ((m % 4) // 2) + late * ((i - 14 + 30) // 3 - 10))
-        near_kind = (1 - foreign) * (i // 5)
-        pair = (1 - foreign) * (i % 5) + foreign * (
-            (1 - late) * (m % 2) + late * (2 + (i - 14 + 30) % 3)
-        )
-        relation = kind + near_kind
+        relation = (1 - foreign) * (i // 5) + foreign * (2 + i % 2)
+        pair = (1 - foreign) * (i % 5) + foreign * (i // 2 - 5)
         lo = (dp + relation) % 2
         hi = (dp // 2 + relation // 2) % 2
         return (2 * hi + lo) * 5 + pair
@@ -374,8 +358,7 @@
     def map_lanes(g, at, base):
         return act[base + g // 2, at, pl.ds(pl.multiple_of((g % 2) * 128, 128), 128)]
 
-    def state_send(r, half):
-        peer = (ctx + r) % 32
+    def state_send(peer, half):
         rows = slice(half * 64, half * 64 + 64)
         return remote(
             state_out.at[peer, rows], state_in.at[half, ctx],
@@ -395,7 +378,8 @@
 
     @pl.loop(0, GROUPS)
     @jax.named_scope("groups")
-    def _(g):
+    def _(n):
+        g = (n + ctx // 8) % 4
         decays = widen(misc_ref[...], g)
         total = None
         for k in range(2):
@@ -414,11 +398,19 @@
         for i in range(8):
             state_out[g * 8 + i] = total[:, i * 128 : (i + 1) * 128].astype(BF16)
 
+        @pl.loop(0, 8)
+        def _(m):
+            peer = g * 8 + (m + ctx) % 8
+
+            @pl.when(peer != ctx)
+            def _():
+                state_send(peer, 0).start()
+
+    @pl.loop(1, 32)
+    def _(r):
+        state_send((ctx + r) % 32, 1).start()
+
     for half in range(2):
-        @pl.loop(1, 32)
-        def _(r):
-            state_send(r, half).start()
-
         state_in[half, ctx] = state_out[ctx, half * 64 : half * 64 + 64]
 
     lane = lax.broadcasted_iota(jnp.int32, (BLOCK, 128), 1) < HEAD_DIM
@@ -426,9 +418,8 @@
         jnp.int32, (128, 128), 1
     )
 
-    @pl.loop(0, 8)
     @jax.named_scope("within")
-    def _(n):
+    def within(n):
         g = n // 2
         start = (n % 2) * BLOCK
         rows = pl.ds(pl.multiple_of(start, BLOCK), BLOCK)
@@ -466,6 +457,8 @@
                 mixed + skip[:, i * 128 : (i + 1) * 128] * values.astype(F32)
             )
 
+    pl.loop(0, 5)(within)
+
     with jax.named_scope("totals"):
         wait_all(totals.at[0:31], 1)
     mine = lax.broadcasted_iota(jnp.int32, (128, 128), 0) % HEADS == (
@@ -491,28 +484,38 @@
 
         enter_in[ctx, half * 64 : half * 64 + 64] = enter_out[half, ctx]
 
+        if half == 0:
+            pl.loop(5, 8)(within)
+
     for half in range(2):
         with jax.named_scope("enterwait"):
             wait_all(enter_in.at[0:31, half * 64 : half * 64 + 64], 8 + half)
 
-    def out_copy(g):
+    def out_copy(g, k):
         columns = pl.ds(pl.multiple_of(g * 1024, 1024), 1024)
-        return pltpu.make_async_copy(mixed_out.at[g], out_ref.at[:, columns], out_sem)
+        rows = slice(k * BLOCK, (k + 1) * BLOCK)
+        return pltpu.make_async_copy(mixed_out.at[g, rows], out_ref.at[rows, columns], out_sem)
 
     @pl.loop(0, GROUPS)
     @jax.named_scope("groups")
     def _(g):
-        decays = widen(misc_ref[...], g)
-        enter = jnp.concatenate([enter_in[g * 8 + i] for i in range(8)], axis=1)
+        decays = widen(misc_ref[...], g)[0:1]
         for k in range(2):
             rows = slice(k * BLOCK, (k + 1) * BLOCK)
-            if k == 1:
-                enter = (decays[0:1] * enter.astype(F32) + first[g]).astype(BF16)
-            carried = jnp.dot(
-                map_lanes(g, rows, 18), enter, preferred_element_type=F32
-            ) * widen(e2_ref[rows], g)
-            mixed_out[g, rows] = (mix[g, rows] + carried).astype(BF16)
-        out_copy(g).start()
+            read = map_lanes(g, rows, 18)
+            for j in range(4):
+                lanes = slice(j * 256, (j + 1) * 256)
+                enter = jnp.concatenate(
+                    [enter_in[g * 8 + 2 * j], enter_in[g * 8 + 2 * j + 1]], axis=1
+                )
+                if k == 1:
+                    enter = decays[:, lanes] * enter.astype(F32) + first[g, :, lanes]
+                    enter = enter.astype(BF16)
+                carried = jnp.dot(read, enter, preferred_element_type=F32) * jnp.dot(
+                    e2_ref[rows], spread[g, :, lanes], preferred_element_type=F32
+                )
+                mixed_out[g, rows, lanes] = (mix[g, rows, lanes] + carried).astype(BF16)
+            out_copy(g, k).start()
 
     with jax.named_scope("drain"):
         halo_copy.wait_send()

time: 86.8 us -> 84.8 us (0.977)
  Pallas kernels: 86.7 us -> 84.5 us
    pallas_call x1, Pallas kernels: 82.2 us -> 80 us  [mixer(): pl.pallas_call(mixer_kernel, out_shape=jax.ShapeDtypeStruct((ROWS, INNER)...]
where the time goes in v4:
time: 84.8 us; the launch traced here: 84.6 us
  Pallas kernels  84.5 us (100%)
    pallas_call x1, Pallas kernels, mixer(): pl.pallas_call(mixer_kernel, out_shape=jax.ShapeDtypeStruct((ROWS, INNER)...  80 us
    pallas_call x1, Pallas kernels, group_norm(): pl.pallas_call(norm_kernel, out_shape=jax.ShapeDtypeStruct((ROWS, INNER),...  4.53 us

profile of v4, /device:TPU:24, one launch (start us, length us, event | category | flops | bytes accessed | tf_op | source)
XLA Modules:
  0.0 84.6 jit_solution(9029671569059168040)
XLA Ops:
  0.0 80.0 %mixer.1.mixed_ref = bf16[512,4096]{1,0:T(8,128)(2,1)} custom-call(bf16[1,512,2048]{2,1,0:T(8,128)(2,1)} %tok_ref.1, bf16[2048,1280]{1,0:T(8,128)(2,1)} %w_ref.1, bf16[64,2048]{1,0:T(8,128)(2,1)} %bitcast.7, f32[1,64]{1,0:T(1,128)} %bitcast.10, f32[1,64]{1,0:T(1,128)} %bitcast.11, f32[1,64]{1,0:T(1,128)} %bitcast.12, f32[4,5120]{1,0:T(4,128)} %taps_ref.1, ...), custom_call_target="tpu_custom_call" | custom-call | tf_op jit(solution)/shard_map/mixer/pallas_call | solution.py:544
  80.0 4.5 %group_norm.1 = bf16[512,4096]{1,0:T(8,128)(2,1)} custom-call(bf16[512,4096]{1,0:T(8,128)(2,1)} %mixer.1.mixed_ref, f32[1,4096]{1,0:T(1,128)} %bitcast.9), custom_call_target="tpu_custom_call" | custom-call | tf_op jit(solution)/shard_map/group_norm/pallas_call | solution.py:595

commit v5 on v4

--- a/solution.py
+++ b/solution.py
@@ -42,9 +42,9 @@
     out_ref,
     tok, wbuf, pbuf, act, swp, small,
     a_ref, bt_ref, lt_ref, w2_ref, e2_ref, misc_ref,
-    spread, first, mix, mixed_out, scores, totals, decays_in,
+    spread, first, mix, scores, totals, decays_in,
     state_out, state_in, enter_out, enter_in,
-    loc_sem, tok_sem, out_sem, halo_sem, sib_send, sib_recv,
+    near_sem, tok_sem, halo_sem, sib_send,
     x_send, x_recv, ring_send, ring_recv, fwd_send, fwd_recv, sems,
 ):
     dp = lax.axis_index("dp")
@@ -65,10 +65,19 @@
     source_b = (across, (ctx + 16) % 32)
     after = (dp, (ctx + 1) % 32)
 
+    low, high = dp % 2, dp // 2
+
+    def own_columns(column):
+        pair = column // 2
+        block = (
+            (1 - low) * pair
+            + low * (1 - high) * ((pair + 3) % 5)
+            + low * high * (1, 2, 0, 3, 4)[pair]
+        )
+        return pl.ds(pl.multiple_of(block * 256 + column % 2 * 128, 128), 128)
+
     def loc_copy(j):
-        return pltpu.make_async_copy(
-            w_ref.at[:, j * 128 : (j + 1) * 128], wbuf.at[j], loc_sem.at[j]
-        )
+        return pltpu.make_async_copy(w_ref.at[:, own_columns(j)], wbuf.at[j], near_sem.at[j])
 
     barrier = pltpu.get_barrier_semaphore()
     for peer in ((sibling, ctx), source_a, source_b):
@@ -95,7 +104,7 @@
         column = RING_COL[dim][p]
         rows = pl.ds(pl.multiple_of(place[dim] * 512, 512), 512)
         return remote(
-            w_ref.at[rows, column * 128 : (column + 1) * 128],
+            w_ref.at[rows, own_columns(column)],
             wbuf.at[same_slot(column), rows],
             x_send.at[dim * 4 + p], x_recv.at[dim * 4 + p],
             source_a if p < 2 else source_b,
@@ -104,7 +113,7 @@
     def x_direct(k):
         column = 8 + k
         return remote(
-            w_ref.at[:, column * 128 : (column + 1) * 128],
+            w_ref.at[:, own_columns(column)],
             wbuf.at[same_slot(column)],
             x_send.at[8 + k], x_recv.at[8 + k], (source_a, source_b)[k],
         )
@@ -147,8 +156,8 @@
 
     def sib_copy(j):
         return remote(
-            w_ref.at[:, j * 128 : (j + 1) * 128], wbuf.at[10 + j],
-            sib_send.at[j], sib_recv.at[j], (sibling, ctx),
+            w_ref.at[:, own_columns(j)], wbuf.at[10 + j],
+            sib_send.at[j], near_sem.at[10 + j], (sibling, ctx),
         )
 
     halo_copy = remote(
@@ -274,41 +283,36 @@
     three = ((0, 1), (1, 3))
     four = ((1, 1), (0, 3))
 
-    def events(i):
-        for n in range(5):
-            @pl.when(i == n)
-            def _(n=n):
-                loc_copy(2 * n).wait()
-                loc_copy(2 * n + 1).wait()
-
-            @pl.when(i == 5 + n)
-            def _(n=n):
-                sib_copy(2 * n).wait_recv()
-                sib_copy(2 * n + 1).wait_recv()
-
-        def at(step, *actions):
-            @pl.when(i == step)
-            def _():
-                for action, pieces in actions:
-                    for piece in pieces:
-                        action(*piece)
-
-        def other(pieces):
-            other_wait(pieces)
-
-        at(2, (x_arrive, one))
-        at(5, (x_arrive, two))
-        at(7, (near_arrive, one))
-        at(8, (x_arrive, three))
-        at(9, (near_arrive, two))
-        at(10, (x_arrive, four), (far_arrive, one))
-        at(11, (near_arrive, three), (other, ((one,),)))
-        at(12, (far_arrive, two))
-        at(13, (near_arrive, four), (other, ((two,),)))
-        at(14, (far_arrive, three))
-        at(15, (other, ((three,),)))
-        at(16, (far_arrive, four), (direct_arrive, ((0,), (1,))))
-        at(17, (other, ((four,),)))
+    def at(i, step, *actions):
+        @pl.when(i == step)
+        def _():
+            for action, pieces in actions:
+                for piece in pieces:
+                    action(*piece)
+
+    def other(pieces):
+        other_wait(pieces)
+
+    def near_events(i):
+        for j in (2 * i, 2 * i + 1):
+            pltpu.make_async_copy(wbuf.at[j], wbuf.at[j], near_sem.at[j]).wait()
+        at(i, 2, (x_arrive, one))
+        at(i, 5, (x_arrive, two))
+        at(i, 7, (near_arrive, one))
+        at(i, 8, (x_arrive, three))
+        at(i, 9, (near_arrive, two))
+
+    def early_events(i):
+        at(i, 10, (x_arrive, four), (far_arrive, one))
+        at(i, 11, (near_arrive, three), (other, ((one,),)))
+        at(i, 12, (far_arrive, two))
+        at(i, 13, (near_arrive, four), (other, ((two,),)))
+
+    def late_events(i):
+        at(i, 14, (far_arrive, three))
+        at(i, 15, (other, ((three,),)))
+        at(i, 16, (far_arrive, four), (direct_arrive, ((0,), (1,))))
+        at(i, 17, (other, ((four,),)))
 
         @pl.when(i == 19)
         def _():
@@ -319,12 +323,17 @@
         foreign = i // 10
         relation = (1 - foreign) * (i // 5) + foreign * (2 + i % 2)
         pair = (1 - foreign) * (i % 5) + foreign * (i // 2 - 5)
-        lo = (dp + relation) % 2
-        hi = (dp // 2 + relation // 2) % 2
-        return (2 * hi + lo) * 5 + pair
-
-    @pl.loop(0, 20)
-    def _(i):
+        slow = (low + relation) % 2
+        shigh = (high + relation // 2) % 2
+        late = pair // 3
+        block = (
+            (1 - slow) * pair
+            + slow * (1 - shigh) * ((pair + 3) % 5)
+            + slow * shigh * (late * pair + (1 - late) * ((pair + 1) % 3))
+        )
+        return (2 * shigh + slow) * 5 + block
+
+    def project(events, i):
         with jax.named_scope("events"):
             events(i)
         with jax.named_scope("compute"):
@@ -358,60 +367,68 @@
     def map_lanes(g, at, base):
         return act[base + g // 2, at, pl.ds(pl.multiple_of((g % 2) * 128, 128), 128)]
 
-    def state_send(peer, half):
-        rows = slice(half * 64, half * 64 + 64)
+    def group_at(stage, m):
+        return (1 - high) * (2 * stage + m) + high * (m if stage else 3 - m)
+
+    def state_send(peer, stage):
         return remote(
-            state_out.at[peer, rows], state_in.at[half, ctx],
-            sems.at[2 + half], sems.at[4 + half], (dp, peer),
-        )
-
-    def enter_send(r, half):
+            state_out.at[stage, peer], state_in.at[stage, ctx],
+            sems.at[2 + stage], sems.at[4 + stage], (dp, peer),
+        )
+
+    def enter_send(r, stage):
         peer = (ctx + r) % 32
-        rows = slice(half * 64, half * 64 + 64)
+        rows = pl.ds(pl.multiple_of((ctx % 2) * 64, 64), 64)
         return remote(
-            enter_out.at[half, peer], enter_in.at[ctx, rows],
-            sems.at[6 + half], sems.at[8 + half], (dp, peer),
+            enter_out.at[stage, peer], enter_in.at[stage * 16 + ctx // 2, rows],
+            sems.at[6 + stage], sems.at[8 + stage], (dp, peer),
         )
 
     def wait_all(part, index):
         pltpu.make_async_copy(part, part, sems.at[index]).wait()
 
-    @pl.loop(0, GROUPS)
-    @jax.named_scope("groups")
-    def _(n):
-        g = (n + ctx // 8) % 4
-        decays = widen(misc_ref[...], g)
-        total = None
-        for k in range(2):
-            at = slice(k * BLOCK, (k + 1) * BLOCK)
-            values = group_of(g, at).astype(F32)
-            scaled = (widen(w2_ref[at], g) * values).astype(BF16)
-            maps = map_lanes(g, at, 16)
-            state = lax.dot_general(
-                maps, scaled, (((0,), (0,)), ((), ())), preferred_element_type=F32
-            )
-            if k == 0:
-                first[g] = state
-                total = decays[1:2] * state
-            else:
-                total = total + state
-        for i in range(8):
-            state_out[g * 8 + i] = total[:, i * 128 : (i + 1) * 128].astype(BF16)
-
-        @pl.loop(0, 8)
-        def _(m):
-            peer = g * 8 + (m + ctx) % 8
-
-            @pl.when(peer != ctx)
-            def _():
-                state_send(peer, 0).start()
-
-    @pl.loop(1, 32)
-    def _(r):
-        state_send((ctx + r) % 32, 1).start()
-
-    for half in range(2):
-        state_in[half, ctx] = state_out[ctx, half * 64 : half * 64 + 64]
+    def states(stage):
+        @pl.loop(0, 2)
+        @jax.named_scope("states")
+        def _(n):
+            m = (n + xh) % 2
+            g = group_at(stage, m)
+            decays = widen(misc_ref[...], g)
+            total = None
+            for k in range(2):
+                at = slice(k * BLOCK, (k + 1) * BLOCK)
+                values = group_of(g, at).astype(F32)
+                scaled = (widen(w2_ref[at], g) * values).astype(BF16)
+                maps = map_lanes(g, at, 16)
+                state = lax.dot_general(
+                    maps, scaled, (((0,), (0,)), ((), ())), preferred_element_type=F32
+                )
+                if k == 0:
+                    first[g] = state
+                    total = decays[1:2] * state
+                else:
+                    total = total + state
+            for i in range(8):
+                for half in range(2):
+                    state_out[stage, 16 * m + 2 * i + half] = total[
+                        half * 64 : half * 64 + 64, i * 128 : (i + 1) * 128
+                    ].astype(BF16)
+
+            @pl.loop(0, 16)
+            def _(j):
+                peer = 16 * m + (j + ctx) % 16
+
+                @pl.when(peer != ctx)
+                def _():
+                    state_send(peer, stage).start()
+
+        state_in[stage, ctx] = state_out[stage, ctx]
+
+    pl.loop(0, 10)(functools.partial(project, near_events))
+    pl.loop(10, 14)(functools.partial(project, early_events))
+    states(0)
+    pl.loop(14, 20)(functools.partial(project, late_events))
+    states(1)
 
     lane = lax.broadcasted_iota(jnp.int32, (BLOCK, 128), 1) < HEAD_DIM
     causal = lax.broadcasted_iota(jnp.int32, (128, 128), 0) >= lax.broadcasted_iota(
@@ -457,65 +474,61 @@
                 mixed + skip[:, i * 128 : (i + 1) * 128] * values.astype(F32)
             )
 
-    pl.loop(0, 5)(within)
-
-    with jax.named_scope("totals"):
-        wait_all(totals.at[0:31], 1)
-    mine = lax.broadcasted_iota(jnp.int32, (128, 128), 0) % HEADS == (
-        2 * ctx + lax.broadcasted_iota(jnp.int32, (128, 128), 1) // HEAD_DIM
-    )
-    pick = mine.astype(F32).astype(BF16)
-    for k in range(32):
-        decays_in[k] = jnp.dot(totals[k], pick, preferred_element_type=F32)
-
-    for half in range(2):
+    def turn(stage):
+        group = group_at(stage, ctx // 16)
+        head = 16 * group + 2 * (ctx // 2 % 8)
+        mine = lax.broadcasted_iota(jnp.int32, (128, 128), 0) % HEADS == (
+            head + lax.broadcasted_iota(jnp.int32, (128, 128), 1) // HEAD_DIM
+        )
+        pick = mine.astype(F32).astype(BF16)
+        for k in range(32):
+            decays_in[k] = jnp.dot(totals[k], pick, preferred_element_type=F32)
         with jax.named_scope("statewait"):
-            wait_all(state_in.at[half, 0:31], 4 + half)
+            wait_all(state_in.at[stage, 0:31], 4 + stage)
 
         def scan(k, carry):
-            enter_out[half, k] = carry.astype(BF16)
-            return decays_in[k, 2:3] * carry + state_in[half, k].astype(F32)
+            enter_out[stage, k] = carry.astype(BF16)
+            return decays_in[k, 2:3] * carry + state_in[stage, k].astype(F32)
 
         lax.fori_loop(0, 32, scan, jnp.zeros((64, 128), F32))
 
         @pl.loop(1, 32)
         def _(r):
-            enter_send(r, half).start()
-
-        enter_in[ctx, half * 64 : half * 64 + 64] = enter_out[half, ctx]
-
-        if half == 0:
-            pl.loop(5, 8)(within)
-
-    for half in range(2):
+            enter_send(r, stage).start()
+
+        rows = pl.ds(pl.multiple_of((ctx % 2) * 64, 64), 64)
+        enter_in[stage * 16 + ctx // 2, rows] = enter_out[stage, ctx]
+
+    wait_all(totals.at[0:31], 1)
+    turn(0)
+    pl.loop(0, 6)(within)
+    turn(1)
+    pl.loop(6, 8)(within)
+
+    for stage in range(2):
         with jax.named_scope("enterwait"):
-            wait_all(enter_in.at[0:31, half * 64 : half * 64 + 64], 8 + half)
-
-    def out_copy(g, k):
-        columns = pl.ds(pl.multiple_of(g * 1024, 1024), 1024)
-        rows = slice(k * BLOCK, (k + 1) * BLOCK)
-        return pltpu.make_async_copy(mixed_out.at[g, rows], out_ref.at[rows, columns], out_sem)
-
-    @pl.loop(0, GROUPS)
-    @jax.named_scope("groups")
-    def _(g):
-        decays = widen(misc_ref[...], g)[0:1]
-        for k in range(2):
-            rows = slice(k * BLOCK, (k + 1) * BLOCK)
-            read = map_lanes(g, rows, 18)
-            for j in range(4):
-                lanes = slice(j * 256, (j + 1) * 256)
-                enter = jnp.concatenate(
-                    [enter_in[g * 8 + 2 * j], enter_in[g * 8 + 2 * j + 1]], axis=1
-                )
-                if k == 1:
-                    enter = decays[:, lanes] * enter.astype(F32) + first[g, :, lanes]
-                    enter = enter.astype(BF16)
-                carried = jnp.dot(read, enter, preferred_element_type=F32) * jnp.dot(
-                    e2_ref[rows], spread[g, :, lanes], preferred_element_type=F32
-                )
-                mixed_out[g, rows, lanes] = (mix[g, rows, lanes] + carried).astype(BF16)
-            out_copy(g, k).start()
+            wait_all(enter_in.at[0:31, 0:64], 8 + stage)
+
+        @pl.loop(0, 2)
+        @jax.named_scope("groups")
+        def _(m):
+            g = group_at(stage, m)
+            decays = widen(misc_ref[...], g)[0:1]
+            for k in range(2):
+                rows = slice(k * BLOCK, (k + 1) * BLOCK)
+                read = map_lanes(g, rows, 18)
+                for j in range(4):
+                    lanes = slice(j * 256, (j + 1) * 256)
+                    pair = stage * 16 + 8 * m + 2 * j
+                    enter = jnp.concatenate([enter_in[pair], enter_in[pair + 1]], axis=1)
+                    if k == 1:
+                        enter = decays[:, lanes] * enter.astype(F32) + first[g, :, lanes]
+                        enter = enter.astype(BF16)
+                    carried = jnp.dot(read, enter, preferred_element_type=F32) * jnp.dot(
+                        e2_ref[rows], spread[g, :, lanes], preferred_element_type=F32
+                    )
+                    columns = pl.ds(pl.multiple_of(g * 1024 + j * 256, 256), 256)
+                    out_ref[rows, columns] = (mix[g, rows, lanes] + carried).astype(BF16)
 
     with jax.named_scope("drain"):
         halo_copy.wait_send()
@@ -534,7 +547,6 @@
         for half in range(2):
             wait_all(state_in.at[half, 0:31], 2 + half)
             wait_all(state_in.at[half, 0:31], 6 + half)
-        pltpu.make_async_copy(mixed_out, mixed_out, out_sem).wait()
 
 
 def mixer(tokens, in_weight, step_weight, bias, rate, skip, taps, filter_bias):
@@ -543,9 +555,9 @@
     dma = pltpu.SemaphoreType.DMA
     return pl.pallas_call(
         mixer_kernel,
-        out_shape=jax.ShapeDtypeStruct((ROWS, INNER), BF16),
+        out_shape=pltpu.VMEM((ROWS, INNER), BF16),
         in_specs=[anywhere, anywhere] + [vmem] * 6,
-        out_specs=anywhere,
+        out_specs=vmem,
         scratch_shapes=[
             pltpu.VMEM((HALO + ROWS, D), BF16),
             pltpu.VMEM((40, D, 128), BF16),
@@ -562,45 +574,52 @@
             pltpu.VMEM((GROUPS, 128, 1024), BF16),
             pltpu.VMEM((GROUPS, STATE, 1024), F32),
             pltpu.VMEM((GROUPS, ROWS, 1024), F32),
-            pltpu.VMEM((GROUPS, ROWS, 1024), BF16),
             pltpu.VMEM((3, 128, 128), F32),
             pltpu.VMEM((32, 8, 128), BF16),
             pltpu.VMEM((32, 8, 128), F32),
-            pltpu.VMEM((32, STATE, 128), BF16),
+            pltpu.VMEM((2, 32, 64, 128), BF16),
             pltpu.VMEM((2, 32, 64, 128), BF16),
             pltpu.VMEM((2, 32, 64, 128), BF16),
             pltpu.VMEM((32, STATE, 128), BF16),
-            dma((10,)), dma, dma, dma((2,)), dma((10,)), dma((10,)),
+            dma((20,)), dma, dma((2,)), dma((10,)),
             dma((10,)), dma((10,)), dma((24,)), dma((24,)), dma((34,)), dma((34,)), dma((10,)),
         ],
         compiler_params=pltpu.CompilerParams(
-            collective_id=0, has_side_effects=True, vmem_limit_bytes=58 * 2**20
+            collective_id=0, has_side_effects=True, vmem_limit_bytes=54 * 2**20
         ),
         name="mixer",
     )(tokens, in_weight, step_weight, bias, rate, skip, taps, filter_bias)
 
 
-def norm_kernel(mixed_ref, gain_ref, out_ref):
-    for g in range(GROUPS):
-        columns = slice(g * 1024, (g + 1) * 1024)
-        mixed = mixed_ref[:, columns].astype(F32)
-        mean = jnp.mean(mixed * mixed, axis=1, keepdims=True)
-        out_ref[:, columns] = (mixed * lax.rsqrt(mean + 1e-05) * gain_ref[:, columns]).astype(
-            BF16
-        )
+def norm_kernel(mixed_ref, gain_ref, out_ref, rows_out, sem):
+    tile = 64
+
+    def copy(n):
+        rows = slice(n * tile, (n + 1) * tile)
+        return pltpu.make_async_copy(rows_out.at[rows], out_ref.at[rows], sem.at[n])
+
+    for n in range(ROWS // tile):
+        rows = slice(n * tile, (n + 1) * tile)
+        for g in range(GROUPS):
+            columns = slice(g * 1024, (g + 1) * 1024)
+            mixed = mixed_ref[rows, columns].astype(F32)
+            mean = jnp.mean(mixed * mixed, axis=1, keepdims=True)
+            normed = mixed * lax.rsqrt(mean + 1e-05) * gain_ref[:, columns]
+            rows_out[rows, columns] = normed.astype(BF16)
+        copy(n).start()
+    for n in range(ROWS // tile):
+        copy(n).wait()
 
 
 def group_norm(mixed, gain):
-    tile = 256
+    vmem = pl.BlockSpec(memory_space=pltpu.VMEM)
     return pl.pallas_call(
         norm_kernel,
         out_shape=jax.ShapeDtypeStruct((ROWS, INNER), BF16),
-        grid=(ROWS // tile,),
-        in_specs=[
-            pl.BlockSpec((tile, INNER), lambda i: (i, 0)),
-            pl.BlockSpec((1, INNER), lambda i: (0, 0)),
-        ],
-        out_specs=pl.BlockSpec((tile, INNER), lambda i: (i, 0)),
+        in_specs=[vmem, vmem],
+        out_specs=pl.BlockSpec(memory_space=pl.ANY),
+        scratch_shapes=[pltpu.VMEM((ROWS, INNER), BF16), pltpu.SemaphoreType.DMA((8,))],
+        compiler_params=pltpu.CompilerParams(vmem_limit_bytes=24 * 2**20),
         name="group_norm",
     )(mixed, gain)
 

time: 84.8 us -> 74.5 us (0.88)
  Pallas kernels: 84.5 us -> 74.4 us
    pallas_call x1, Pallas kernels: 80 us -> 71.8 us  [mixer(): pl.pallas_call(mixer_kernel, out_shape=pltpu.VMEM((ROWS, INNER), BF16), i...]
    pallas_call x1, Pallas kernels: 4.53 us -> 2.6 us  [group_norm(): pl.pallas_call(norm_kernel, out_shape=jax.ShapeDtypeStruct((ROWS, INNER),...]
where the time goes in v5:
time: 74.5 us; the launch traced here: 74.4 us
  Pallas kernels  74.4 us (100%)
    pallas_call x1, Pallas kernels, mixer(): pl.pallas_call(mixer_kernel, out_shape=pltpu.VMEM((ROWS, INNER), BF16), i...  71.8 us
    pallas_call x1, Pallas kernels, group_norm(): pl.pallas_call(norm_kernel, out_shape=jax.ShapeDtypeStruct((ROWS, INNER),...  2.6 us

profile of v5, /device:TPU:24, one launch (start us, length us, event | category | flops | bytes accessed | tf_op | source)
XLA Modules:
  0.0 74.4 jit_solution(10385431107227880436)
XLA Ops:
  0.0 0.0 copy-start
  0.0 71.8 %mixer.1.mixed_ref = bf16[512,4096]{1,0:T(8,128)(2,1)S(1)} custom-call(bf16[1,512,2048]{2,1,0:T(8,128)(2,1)} %tok_ref.1, bf16[2048,1280]{1,0:T(8,128)(2,1)} %w_ref.1, bf16[64,2048]{1,0:T(8,128)(2,1)} %bitcast.8, f32[1,64]{1,0:T(1,128)} %bitcast.10, f32[1,64]{1,0:T(1,128)} %bitcast.11, f32[1,64]{1,0:T(1,128)} %bitcast.12, f32[4,5120]{1,0:T(4,128)} %taps_ref.1, ...), custom_call_target="tpu_custom_call" | custom-call | tf_op jit(solution)/shard_map/mixer/pallas_call | solution.py:556
  71.8 0.0 copy-done
  71.8 2.6 %group_norm.1 = bf16[512,4096]{1,0:T(8,128)(2,1)} custom-call(bf16[512,4096]{1,0:T(8,128)(2,1)S(1)} %mixer.1.mixed_ref, f32[1,4096]{1,0:T(1,128)S(1)} %bitcast.7), custom_call_target="tpu_custom_call" | custom-call | tf_op jit(solution)/shard_map/group_norm/pallas_call | solution.py:616
Async XLA Ops:
  0.0 71.8 %copy-start = (f32[4096]{0:T(1024)S(1)}, f32[4096]{0:T(1024)}, u32[]{:S(2)}) copy-start(f32[4096]{0:T(1024)} %param.17) | copy-start | bytes 49156

commit v6 on v5

--- a/solution.py
+++ b/solution.py
@@ -43,7 +43,7 @@
     tok, wbuf, pbuf, act, swp, small,
     a_ref, bt_ref, lt_ref, w2_ref, e2_ref, misc_ref,
     spread, first, mix, scores, totals, decays_in,
-    state_out, state_in, enter_out, enter_in,
+    out_0, out_1, out_2, in_0, in_1, in_2, back_0, back_1, back_2, enter_in,
     near_sem, tok_sem, halo_sem, sib_send,
     x_send, x_recv, ring_send, ring_recv, fwd_send, fwd_recv, sems,
 ):
@@ -304,8 +304,8 @@
 
     def early_events(i):
         at(i, 10, (x_arrive, four), (far_arrive, one))
-        at(i, 11, (near_arrive, three), (other, ((one,),)))
-        at(i, 12, (far_arrive, two))
+        at(i, 11, (other, ((one,),)))
+        at(i, 12, (far_arrive, two), (near_arrive, three))
         at(i, 13, (near_arrive, four), (other, ((two,),)))
 
     def late_events(i):
@@ -314,6 +314,7 @@
         at(i, 16, (far_arrive, four), (direct_arrive, ((0,), (1,))))
         at(i, 17, (other, ((four,),)))
 
+    def last_events(i):
         @pl.when(i == 19)
         def _():
             forward(8).wait_recv()
@@ -367,31 +368,45 @@
     def map_lanes(g, at, base):
         return act[base + g // 2, at, pl.ds(pl.multiple_of((g % 2) * 128, 128), 128)]
 
+    state_out, state_in, enter_out = (out_0, out_1, out_2), (in_0, in_1, in_2), (back_0, back_1, back_2)
+    parts, begin = (2, 4, 4), (0, 16, 24)
+
     def group_at(stage, m):
-        return (1 - high) * (2 * stage + m) + high * (m if stage else 3 - m)
+        if stage == 0:
+            return (1 - high) * m + high * (3 - m)
+        return (1 - high) * (1 + stage) + high * (stage - 1)
 
     def state_send(peer, stage):
         return remote(
-            state_out.at[stage, peer], state_in.at[stage, ctx],
-            sems.at[2 + stage], sems.at[4 + stage], (dp, peer),
-        )
+            state_out[stage].at[peer], state_in[stage].at[ctx],
+            sems.at[2 + stage], sems.at[5 + stage], (dp, peer),
+        )
+
+    def my_place(stage):
+        size = STATE // parts[stage]
+        rows = pl.ds(pl.multiple_of(ctx % parts[stage] * size, size), size)
+        return begin[stage] + ctx // parts[stage], rows
 
     def enter_send(r, stage):
         peer = (ctx + r) % 32
-        rows = pl.ds(pl.multiple_of((ctx % 2) * 64, 64), 64)
+        pair, rows = my_place(stage)
         return remote(
-            enter_out.at[stage, peer], enter_in.at[stage * 16 + ctx // 2, rows],
-            sems.at[6 + stage], sems.at[8 + stage], (dp, peer),
+            enter_out[stage].at[peer], enter_in.at[pair, rows],
+            sems.at[8 + stage], sems.at[11 + stage], (dp, peer),
         )
 
     def wait_all(part, index):
         pltpu.make_async_copy(part, part, sems.at[index]).wait()
 
     def states(stage):
-        @pl.loop(0, 2)
+        groups = 1 if stage else 2
+        owners = 32 // groups
+        size = STATE // parts[stage]
+
+        @pl.loop(0, groups)
         @jax.named_scope("states")
         def _(n):
-            m = (n + xh) % 2
+            m = (n + xh) % groups
             g = group_at(stage, m)
             decays = widen(misc_ref[...], g)
             total = None
@@ -409,26 +424,28 @@
                 else:
                     total = total + state
             for i in range(8):
-                for half in range(2):
-                    state_out[stage, 16 * m + 2 * i + half] = total[
-                        half * 64 : half * 64 + 64, i * 128 : (i + 1) * 128
+                for part in range(parts[stage]):
+                    state_out[stage][owners * m + parts[stage] * i + part] = total[
+                        part * size : part * size + size, i * 128 : (i + 1) * 128
                     ].astype(BF16)
 
-            @pl.loop(0, 16)
+            @pl.loop(0, owners)
             def _(j):
-                peer = 16 * m + (j + ctx) % 16
+                peer = owners * m + (j + ctx) % owners
 
                 @pl.when(peer != ctx)
                 def _():
                     state_send(peer, stage).start()
 
-        state_in[stage, ctx] = state_out[stage, ctx]
+        state_in[stage][ctx] = state_out[stage][ctx]
 
     pl.loop(0, 10)(functools.partial(project, near_events))
     pl.loop(10, 14)(functools.partial(project, early_events))
     states(0)
-    pl.loop(14, 20)(functools.partial(project, late_events))
+    pl.loop(14, 18)(functools.partial(project, late_events))
     states(1)
+    pl.loop(18, 20)(functools.partial(project, last_events))
+    states(2)
 
     lane = lax.broadcasted_iota(jnp.int32, (BLOCK, 128), 1) < HEAD_DIM
     causal = lax.broadcasted_iota(jnp.int32, (128, 128), 0) >= lax.broadcasted_iota(
@@ -475,8 +492,9 @@
             )
 
     def turn(stage):
-        group = group_at(stage, ctx // 16)
-        head = 16 * group + 2 * (ctx // 2 % 8)
+        pair, rows = my_place(stage)
+        pair = pair - begin[stage]
+        head = 16 * group_at(stage, pair // 8) + 2 * (pair % 8)
         mine = lax.broadcasted_iota(jnp.int32, (128, 128), 0) % HEADS == (
             head + lax.broadcasted_iota(jnp.int32, (128, 128), 1) // HEAD_DIM
         )
@@ -484,32 +502,33 @@
         for k in range(32):
             decays_in[k] = jnp.dot(totals[k], pick, preferred_element_type=F32)
         with jax.named_scope("statewait"):
-            wait_all(state_in.at[stage, 0:31], 4 + stage)
+            wait_all(state_in[stage].at[0:31], 5 + stage)
 
         def scan(k, carry):
-            enter_out[stage, k] = carry.astype(BF16)
-            return decays_in[k, 2:3] * carry + state_in[stage, k].astype(F32)
-
-        lax.fori_loop(0, 32, scan, jnp.zeros((64, 128), F32))
+            enter_out[stage][k] = carry.astype(BF16)
+            return decays_in[k, 2:3] * carry + state_in[stage][k].astype(F32)
+
+        lax.fori_loop(0, 32, scan, jnp.zeros((STATE // parts[stage], 128), F32))
 
         @pl.loop(1, 32)
         def _(r):
             enter_send(r, stage).start()
 
-        rows = pl.ds(pl.multiple_of((ctx % 2) * 64, 64), 64)
-        enter_in[stage * 16 + ctx // 2, rows] = enter_out[stage, ctx]
+        enter_in[begin[stage] + pair, rows] = enter_out[stage][ctx]
 
     wait_all(totals.at[0:31], 1)
     turn(0)
-    pl.loop(0, 6)(within)
+    pl.loop(0, 2)(within)
     turn(1)
-    pl.loop(6, 8)(within)
-
-    for stage in range(2):
+    pl.loop(2, 5)(within)
+    turn(2)
+    pl.loop(5, 8)(within)
+
+    for stage in range(3):
         with jax.named_scope("enterwait"):
-            wait_all(enter_in.at[0:31, 0:64], 8 + stage)
-
-        @pl.loop(0, 2)
+            wait_all(enter_in.at[0:31, 0 : STATE // parts[stage]], 11 + stage)
+
+        @pl.loop(0, 1 if stage else 2)
         @jax.named_scope("groups")
         def _(m):
             g = group_at(stage, m)
@@ -519,7 +538,7 @@
                 read = map_lanes(g, rows, 18)
                 for j in range(4):
                     lanes = slice(j * 256, (j + 1) * 256)
-                    pair = stage * 16 + 8 * m + 2 * j
+                    pair = begin[stage] + 8 * m + 2 * j
                     enter = jnp.concatenate([enter_in[pair], enter_in[pair + 1]], axis=1)
                     if k == 1:
                         enter = decays[:, lanes] * enter.astype(F32) + first[g, :, lanes]
@@ -544,9 +563,9 @@
         for index in range(34):
             forward(index).wait_send()
         wait_all(totals.at[0:31], 0)
-        for half in range(2):
-            wait_all(state_in.at[half, 0:31], 2 + half)
-            wait_all(state_in.at[half, 0:31], 6 + half)
+        for stage in range(3):
+            wait_all(state_in[stage].at[0:31], 2 + stage)
+            wait_all(state_in[stage].at[0:31], 8 + stage)
 
 
 def mixer(tokens, in_weight, step_weight, bias, rate, skip, taps, filter_bias):
@@ -577,12 +596,10 @@
             pltpu.VMEM((3, 128, 128), F32),
             pltpu.VMEM((32, 8, 128), BF16),
             pltpu.VMEM((32, 8, 128), F32),
-            pltpu.VMEM((2, 32, 64, 128), BF16),
-            pltpu.VMEM((2, 32, 64, 128), BF16),
-            pltpu.VMEM((2, 32, 64, 128), BF16),
+            *[pltpu.VMEM((32, rows, 128), BF16) for rows in (64, 32, 32) * 3],
             pltpu.VMEM((32, STATE, 128), BF16),
             dma((20,)), dma, dma((2,)), dma((10,)),
-            dma((10,)), dma((10,)), dma((24,)), dma((24,)), dma((34,)), dma((34,)), dma((10,)),
+            dma((10,)), dma((10,)), dma((24,)), dma((24,)), dma((34,)), dma((34,)), dma((14,)),
         ],
         compiler_params=pltpu.CompilerParams(
             collective_id=0, has_side_effects=True, vmem_limit_bytes=54 * 2**20

time: 74.5 us -> 71.9 us (0.965)
  Pallas kernels: 74.4 us -> 71.5 us
    pallas_call x1, Pallas kernels: 71.8 us -> 68.9 us  [mixer(): pl.pallas_call(mixer_kernel, out_shape=pltpu.VMEM((ROWS, INNER), BF16), i...]
where the time goes in v6:
time: 71.9 us; the launch traced here: 71.7 us
  Pallas kernels  71.5 us (99%)
    pallas_call x1, Pallas kernels, mixer(): pl.pallas_call(mixer_kernel, out_shape=pltpu.VMEM((ROWS, INNER), BF16), i...  68.9 us
    pallas_call x1, Pallas kernels, group_norm(): pl.pallas_call(norm_kernel, out_shape=jax.ShapeDtypeStruct((ROWS, INNER),...  2.6 us

profile of v6, /device:TPU:24, one launch (start us, length us, event | category | flops | bytes accessed | tf_op | source)
XLA Modules:
  0.0 71.7 jit_solution(26133373097813047)
XLA Ops:
  0.0 0.0 copy-start
  0.0 68.9 %mixer.1.mixed_ref = bf16[512,4096]{1,0:T(8,128)(2,1)S(1)} custom-call(bf16[1,512,2048]{2,1,0:T(8,128)(2,1)} %tok_ref.1, bf16[2048,1280]{1,0:T(8,128)(2,1)} %w_ref.1, bf16[64,2048]{1,0:T(8,128)(2,1)} %bitcast.8, f32[1,64]{1,0:T(1,128)} %bitcast.10, f32[1,64]{1,0:T(1,128)} %bitcast.11, f32[1,64]{1,0:T(1,128)} %bitcast.12, f32[4,5120]{1,0:T(4,128)} %taps_ref.1, ...), custom_call_target="tpu_custom_call" | custom-call | tf_op jit(solution)/shard_map/mixer/pallas_call | solution.py:575
  69.0 0.0 copy-done
  69.0 2.6 %group_norm.1 = bf16[512,4096]{1,0:T(8,128)(2,1)} custom-call(bf16[512,4096]{1,0:T(8,128)(2,1)S(1)} %mixer.1.mixed_ref, f32[1,4096]{1,0:T(1,128)S(1)} %bitcast.7), custom_call_target="tpu_custom_call" | custom-call | tf_op jit(solution)/shard_map/group_norm/pallas_call | solution.py:633
Async XLA Ops:
  0.0 69.0 %copy-start = (f32[4096]{0:T(1024)S(1)}, f32[4096]{0:T(1024)}, u32[]{:S(2)}) copy-start(f32[4096]{0:T(1024)} %param.17) | copy-start | bytes 49156

commit v7 on v6

--- a/solution.py
+++ b/solution.py
@@ -23,7 +23,8 @@
 F32 = jnp.float32
 BF16 = jnp.bfloat16
 
-RING_COL = ((0, 4, 3, 7), (2, 6, 1, 5))
+RING_COL = ((0, 4, 3, 9), (2, 8, 1, 5))
+DIRECT_COL = 6
 SAME_SLOT = (10, 12, 14, 16, 18)
 OTHER_SLOT = (11, 13, 15, 17, 19)
 PEERS = 34
@@ -38,13 +39,14 @@
 
 
 def mixer_kernel(
-    tok_ref, w_ref, sw_ref, bias_ref, rate_ref, skip_ref, taps_ref, fb_ref,
+    tok_ref, w_ref, sw_hbm, bias_hbm, rate_hbm, skip_hbm, taps_hbm, fb_hbm,
     out_ref,
+    taps_ref, fb_ref, bias_ref, rate_ref, skip_ref,
     tok, wbuf, pbuf, act, swp, small,
     a_ref, bt_ref, lt_ref, w2_ref, e2_ref, misc_ref,
     spread, first, mix, scores, totals, decays_in,
     out_0, out_1, out_2, in_0, in_1, in_2, back_0, back_1, back_2, enter_in,
-    near_sem, tok_sem, halo_sem, sib_send,
+    near_sem, tok_sem, small_sem, halo_sem, sib_send,
     x_send, x_recv, ring_send, ring_recv, fwd_send, fwd_recv, sems,
 ):
     dp = lax.axis_index("dp")
@@ -79,6 +81,8 @@
     def loc_copy(j):
         return pltpu.make_async_copy(w_ref.at[:, own_columns(j)], wbuf.at[j], near_sem.at[j])
 
+    loc_copy(0).start()
+    loc_copy(1).start()
     barrier = pltpu.get_barrier_semaphore()
     for peer in ((sibling, ctx), source_a, source_b):
         pl.semaphore_signal(barrier, inc=1, device_id=peer, device_id_type=MESH)
@@ -91,7 +95,16 @@
 
     tok_copy = pltpu.make_async_copy(tok_ref.at[0], tok.at[HALO:], tok_sem)
     tok_copy.start()
-    for j in range(4):
+    small_copies = [
+        pltpu.make_async_copy(src, dst, small_sem.at[n])
+        for n, (src, dst) in enumerate((
+            (sw_hbm, swp.at[0:HEADS]), (bias_hbm, bias_ref), (rate_hbm, rate_ref),
+            (skip_hbm, skip_ref), (taps_hbm, taps_ref), (fb_hbm, fb_ref),
+        ))
+    ]
+    for copy in small_copies:
+        copy.start()
+    for j in range(2, 4):
         loc_copy(j).start()
 
     def remote(src, dst, send, recv, peer):
@@ -103,15 +116,16 @@
     def x_piece(dim, p):
         column = RING_COL[dim][p]
         rows = pl.ds(pl.multiple_of(place[dim] * 512, 512), 512)
+        own = w_ref.at[rows, own_columns(column)] if column > 1 else wbuf.at[column, rows]
         return remote(
-            w_ref.at[rows, own_columns(column)],
+            own,
             wbuf.at[same_slot(column), rows],
             x_send.at[dim * 4 + p], x_recv.at[dim * 4 + p],
             source_a if p < 2 else source_b,
         )
 
     def x_direct(k):
-        column = 8 + k
+        column = DIRECT_COL + k
         return remote(
             w_ref.at[:, own_columns(column)],
             wbuf.at[same_slot(column)],
@@ -140,7 +154,8 @@
 
     def forward(index):
         if index in (8, 9):
-            src, dst = wbuf.at[same_slot(index)], wbuf.at[other_slot(index)]
+            column = DIRECT_COL + index - 8
+            src, dst = wbuf.at[same_slot(column)], wbuf.at[other_slot(column)]
         else:
             if index < 8:
                 dim, p = divmod(index, 4)
@@ -167,6 +182,8 @@
     with jax.named_scope("barrier"):
         pl.semaphore_wait(barrier, PEERS)
     halo_copy.start()
+    loc_copy(0).wait()
+    loc_copy(1).wait()
     for p, q in ((0, 2), (1, 3)):
         x_piece(0, p).start()
         x_piece(1, q).start()
@@ -179,8 +196,9 @@
     for j in range(10):
         sib_copy(j).start()
 
-    swp[...] = jnp.zeros_like(swp)
-    swp[0:HEADS] = sw_ref[...]
+    swp[HEADS:] = jnp.zeros((128 - HEADS, D), BF16)
+    for copy in small_copies:
+        copy.wait()
     small[...] = jnp.zeros_like(small)
     small[0:1, 0:HEADS] = bias_ref[...]
     small[1:2, 0:HEADS] = rate_ref[...]
@@ -293,9 +311,15 @@
     def other(pieces):
         other_wait(pieces)
 
+    def other_direct(index):
+        forward(index).wait_recv()
+
     def near_events(i):
-        for j in (2 * i, 2 * i + 1):
-            pltpu.make_async_copy(wbuf.at[j], wbuf.at[j], near_sem.at[j]).wait()
+        @pl.when(i > 0)
+        def _():
+            for j in (2 * i, 2 * i + 1):
+                pltpu.make_async_copy(wbuf.at[j], wbuf.at[j], near_sem.at[j]).wait()
+
         at(i, 2, (x_arrive, one))
         at(i, 5, (x_arrive, two))
         at(i, 7, (near_arrive, one))
@@ -310,15 +334,12 @@
 
     def late_events(i):
         at(i, 14, (far_arrive, three))
-        at(i, 15, (other, ((three,),)))
-        at(i, 16, (far_arrive, four), (direct_arrive, ((0,), (1,))))
-        at(i, 17, (other, ((four,),)))
+        at(i, 15, (direct_arrive, ((0,), (1,))), (other, ((three,),)))
+        at(i, 17, (other_direct, ((8,), (9,))))
 
     def last_events(i):
-        @pl.when(i == 19)
-        def _():
-            forward(8).wait_recv()
-            forward(9).wait_recv()
+        at(i, 18, (far_arrive, four))
+        at(i, 19, (other, ((four,),)))
 
     def block_of(i):
         foreign = i // 10
@@ -518,9 +539,9 @@
 
     wait_all(totals.at[0:31], 1)
     turn(0)
-    pl.loop(0, 2)(within)
+    pl.loop(0, 4)(within)
     turn(1)
-    pl.loop(2, 5)(within)
+    pl.loop(4, 5)(within)
     turn(2)
     pl.loop(5, 8)(within)
 
@@ -575,9 +596,12 @@
     return pl.pallas_call(
         mixer_kernel,
         out_shape=pltpu.VMEM((ROWS, INNER), BF16),
-        in_specs=[anywhere, anywhere] + [vmem] * 6,
+        in_specs=[anywhere] * 8,
         out_specs=vmem,
         scratch_shapes=[
+            pltpu.VMEM((4, XBC), F32),
+            pltpu.VMEM((1, XBC), F32),
+            *[pltpu.VMEM((1, HEADS), F32) for _ in range(3)],
             pltpu.VMEM((HALO + ROWS, D), BF16),
             pltpu.VMEM((40, D, 128), BF16),
             pltpu.VMEM((2, HALO + ROWS, 128), F32),
@@ -598,7 +622,7 @@
             pltpu.VMEM((32, 8, 128), F32),
             *[pltpu.VMEM((32, rows, 128), BF16) for rows in (64, 32, 32) * 3],
             pltpu.VMEM((32, STATE, 128), BF16),
-            dma((20,)), dma, dma((2,)), dma((10,)),
+            dma((20,)), dma, dma((6,)), dma((2,)), dma((10,)),
             dma((10,)), dma((10,)), dma((24,)), dma((24,)), dma((34,)), dma((34,)), dma((14,)),
         ],
         compiler_params=pltpu.CompilerParams(

time: 71.9 us -> 69.1 us (0.961)
  Pallas kernels: 71.5 us -> 68.5 us
    pallas_call x1, Pallas kernels: 68.9 us -> 65.9 us  [mixer(): pl.pallas_call(mixer_kernel, out_shape=pltpu.VMEM((ROWS, INNER), BF16), i...]
where the time goes in v7:
time: 69.1 us; the launch traced here: 68.6 us
  Pallas kernels  68.5 us (99%)
    pallas_call x1, Pallas kernels, mixer(): pl.pallas_call(mixer_kernel, out_shape=pltpu.VMEM((ROWS, INNER), BF16), i...  65.9 us
    pallas_call x1, Pallas kernels, group_norm(): pl.pallas_call(norm_kernel, out_shape=jax.ShapeDtypeStruct((ROWS, INNER),...  2.6 us

profile of v7, /device:TPU:24, one launch (start us, length us, event | category | flops | bytes accessed | tf_op | source)
XLA Modules:
  0.0 68.6 jit_solution(4128365661379565963)
XLA Ops:
  0.0 0.0 copy-start
  0.0 65.9 %mixer.1.mixed_ref = bf16[512,4096]{1,0:T(8,128)(2,1)S(1)} custom-call(bf16[1,512,2048]{2,1,0:T(8,128)(2,1)} %tok_ref.1, bf16[2048,1280]{1,0:T(8,128)(2,1)} %w_ref.1, bf16[64,2048]{1,0:T(8,128)(2,1)} %bitcast.8, f32[1,64]{1,0:T(1,128)} %bitcast.10, f32[1,64]{1,0:T(1,128)} %bitcast.11, f32[1,64]{1,0:T(1,128)} %bitcast.12, f32[4,5120]{1,0:T(4,128)} %taps_hbm.1, ...), custom_call_target="tpu_custom_call" | custom-call | tf_op jit(solution)/shard_map/mixer/pallas_call | solution.py:596
  65.9 0.0 copy-done
  65.9 2.6 %group_norm.1 = bf16[512,4096]{1,0:T(8,128)(2,1)} custom-call(bf16[512,4096]{1,0:T(8,128)(2,1)S(1)} %mixer.1.mixed_ref, f32[1,4096]{1,0:T(1,128)S(1)} %bitcast.7), custom_call_target="tpu_custom_call" | custom-call | tf_op jit(solution)/shard_map/group_norm/pallas_call | solution.py:657
Async XLA Ops:
  0.0 65.9 %copy-start = (f32[4096]{0:T(1024)S(1)}, f32[4096]{0:T(1024)}, u32[]{:S(2)}) copy-start(f32[4096]{0:T(1024)} %param.17) | copy-start | bytes 49156

commit v8 on v7

--- a/solution.py
+++ b/solution.py
@@ -329,7 +329,7 @@
     def early_events(i):
         at(i, 10, (x_arrive, four), (far_arrive, one))
         at(i, 11, (other, ((one,),)))
-        at(i, 12, (far_arrive, two), (near_arrive, three))
+        at(i, 12, (near_arrive, three), (far_arrive, two))
         at(i, 13, (near_arrive, four), (other, ((two,),)))
 
     def late_events(i):
@@ -418,6 +418,14 @@
 
     def wait_all(part, index):
         pltpu.make_async_copy(part, part, sems.at[index]).wait()
+
+    def fan_out(copy_to):
+        @pl.loop(0, 6)
+        def _(n):
+            for q in range(5):
+                copy_to(5 * n + q + 1).start()
+
+        copy_to(31).start()
 
     def states(stage):
         groups = 1 if stage else 2
@@ -450,13 +458,16 @@
                         part * size : part * size + size, i * 128 : (i + 1) * 128
                     ].astype(BF16)
 
-            @pl.loop(0, owners)
-            def _(j):
-                peer = owners * m + (j + ctx) % owners
-
-                @pl.when(peer != ctx)
-                def _():
-                    state_send(peer, stage).start()
+            if stage:
+                fan_out(lambda r: state_send((ctx + r) % 32, stage))
+            else:
+                @pl.loop(0, owners)
+                def _(j):
+                    peer = owners * m + (j + ctx) % owners
+
+                    @pl.when(peer != ctx)
+                    def _():
+                        state_send(peer, stage).start()
 
         state_in[stage][ctx] = state_out[stage][ctx]
 
@@ -525,21 +536,22 @@
         with jax.named_scope("statewait"):
             wait_all(state_in[stage].at[0:31], 5 + stage)
 
-        def scan(k, carry):
-            enter_out[stage][k] = carry.astype(BF16)
-            return decays_in[k, 2:3] * carry + state_in[stage][k].astype(F32)
-
-        lax.fori_loop(0, 32, scan, jnp.zeros((STATE // parts[stage], 128), F32))
-
-        @pl.loop(1, 32)
-        def _(r):
-            enter_send(r, stage).start()
+        def scan(n, carry):
+            for k in range(4):
+                enter_out[stage][4 * n + k] = carry.astype(BF16)
+                here = state_in[stage][4 * n + k].astype(F32)
+                carry = decays_in[4 * n + k, 2:3] * carry + here
+            return carry
+
+        lax.fori_loop(0, 8, scan, jnp.zeros((STATE // parts[stage], 128), F32))
+        fan_out(lambda r: enter_send(r, stage))
 
         enter_in[begin[stage] + pair, rows] = enter_out[stage][ctx]
 
     wait_all(totals.at[0:31], 1)
+    pl.loop(0, 1)(within)
     turn(0)
-    pl.loop(0, 4)(within)
+    pl.loop(1, 4)(within)
     turn(1)
     pl.loop(4, 5)(within)
     turn(2)

time: 69.1 us -> 68.3 us (0.988)
  no operation moved by 1% of the time
where the time goes in v8:
time: 68.3 us; the launch traced here: 68.2 us
  Pallas kernels  68 us (100%)
    pallas_call x1, Pallas kernels, mixer(): pl.pallas_call(mixer_kernel, out_shape=pltpu.VMEM((ROWS, INNER), BF16), i...  65.4 us
    pallas_call x1, Pallas kernels, group_norm(): pl.pallas_call(norm_kernel, out_shape=jax.ShapeDtypeStruct((ROWS, INNER),...  2.6 us

profile of v8, /device:TPU:24, one launch (start us, length us, event | category | flops | bytes accessed | tf_op | source)
XLA Modules:
  0.0 68.2 jit_solution(1985616500527072252)
XLA Ops:
  0.0 0.0 copy-start
  0.0 65.4 %mixer.1.mixed_ref = bf16[512,4096]{1,0:T(8,128)(2,1)S(1)} custom-call(bf16[1,512,2048]{2,1,0:T(8,128)(2,1)} %tok_ref.1, bf16[2048,1280]{1,0:T(8,128)(2,1)} %w_ref.1, bf16[64,2048]{1,0:T(8,128)(2,1)} %bitcast.8, f32[1,64]{1,0:T(1,128)} %bitcast.10, f32[1,64]{1,0:T(1,128)} %bitcast.11, f32[1,64]{1,0:T(1,128)} %bitcast.12, f32[4,5120]{1,0:T(4,128)} %taps_hbm.1, ...), custom_call_target="tpu_custom_call" | custom-call | tf_op jit(solution)/shard_map/mixer/pallas_call | solution.py:608
  65.4 0.0 copy-done
  65.4 2.6 %group_norm.1 = bf16[512,4096]{1,0:T(8,128)(2,1)} custom-call(bf16[512,4096]{1,0:T(8,128)(2,1)S(1)} %mixer.1.mixed_ref, f32[1,4096]{1,0:T(1,128)S(1)} %bitcast.7), custom_call_target="tpu_custom_call" | custom-call | tf_op jit(solution)/shard_map/group_norm/pallas_call | solution.py:669
Async XLA Ops:
  0.0 65.4 %copy-start = (f32[4096]{0:T(1024)S(1)}, f32[4096]{0:T(1024)}, u32[]{:S(2)}) copy-start(f32[4096]{0:T(1024)} %param.17) | copy-start | bytes 49156

commit v9 on v8

--- a/solution.py
+++ b/solution.py
@@ -461,13 +461,19 @@
             if stage:
                 fan_out(lambda r: state_send((ctx + r) % 32, stage))
             else:
-                @pl.loop(0, owners)
-                def _(j):
-                    peer = owners * m + (j + ctx) % owners
-
-                    @pl.when(peer != ctx)
-                    def _():
-                        state_send(peer, stage).start()
+                @pl.when(n == 0)
+                def _():
+                    @pl.loop(0, 3)
+                    def _(b):
+                        for q in range(5):
+                            state_send(16 * m + (ctx + 5 * b + q + 1) % 16, stage).start()
+
+                @pl.when(n == 1)
+                def _():
+                    @pl.loop(0, 4)
+                    def _(b):
+                        for q in range(4):
+                            state_send(16 * m + (ctx + 4 * b + q) % 16, stage).start()
 
         state_in[stage][ctx] = state_out[stage][ctx]
 

time: 68.3 us -> 68.3 us (level)
  no operation moved by 1% of the time
where the time goes in v9:
time: 68.3 us; the launch traced here: 67.8 us
  Pallas kernels  67.7 us (99%)
    pallas_call x1, Pallas kernels, mixer(): pl.pallas_call(mixer_kernel, out_shape=pltpu.VMEM((ROWS, INNER), BF16), i...  65.1 us
    pallas_call x1, Pallas kernels, group_norm(): pl.pallas_call(norm_kernel, out_shape=jax.ShapeDtypeStruct((ROWS, INNER),...  2.6 us

profile of v9, /device:TPU:24, one launch (start us, length us, event | category | flops | bytes accessed | tf_op | source)
XLA Modules:
  0.0 67.8 jit_solution(17845013385670056642)
XLA Ops:
  0.0 0.0 copy-start
  0.0 65.1 %mixer.1.mixed_ref = bf16[512,4096]{1,0:T(8,128)(2,1)S(1)} custom-call(bf16[1,512,2048]{2,1,0:T(8,128)(2,1)} %tok_ref.1, bf16[2048,1280]{1,0:T(8,128)(2,1)} %w_ref.1, bf16[64,2048]{1,0:T(8,128)(2,1)} %bitcast.8, f32[1,64]{1,0:T(1,128)} %bitcast.10, f32[1,64]{1,0:T(1,128)} %bitcast.11, f32[1,64]{1,0:T(1,128)} %bitcast.12, f32[4,5120]{1,0:T(4,128)} %taps_hbm.1, ...), custom_call_target="tpu_custom_call" | custom-call | tf_op jit(solution)/shard_map/mixer/pallas_call | solution.py:614
  65.1 0.0 copy-done
  65.1 2.6 %group_norm.1 = bf16[512,4096]{1,0:T(8,128)(2,1)} custom-call(bf16[512,4096]{1,0:T(8,128)(2,1)S(1)} %mixer.1.mixed_ref, f32[1,4096]{1,0:T(1,128)S(1)} %bitcast.7), custom_call_target="tpu_custom_call" | custom-call | tf_op jit(solution)/shard_map/group_norm/pallas_call | solution.py:675
Async XLA Ops:
  0.0 65.1 %copy-start = (f32[4096]{0:T(1024)S(1)}, f32[4096]{0:T(1024)}, u32[]{:S(2)}) copy-start(f32[4096]{0:T(1024)} %param.17) | copy-start | bytes 49156
